TPU v7x, 32 devices: a 4x4x1 block of a 4x4x8 slice. The times are simulated.
32 devices in a mesh: dp: 1 (over z), gz: 4 (over y), gy: 4 (over x), gx: 2 (over core).
Axes of the slice: x: 4, y: 4, z: 1, core: 2. Of those that a mesh axis runs over, the one named last changes fastest.
The devices are a block of a 4x4x8 slice.
Arguments:
- volume: bfloat16 [256, 32, 64, 64], P('dp', 'gx', 'gy', 'gz')
- cot_out: bfloat16 [256, 32, 64, 64], P('dp', 'gx', 'gy', 'gz')
- filter_taps: float32 [3, 3, 5], replicated
- w_mix: bfloat16 [3, 256, 256], replicated
- b_mix: float32 [3, 256], replicated
Outputs:
- output 1: bfloat16 [256, 32, 64, 64], P('dp', 'gx', 'gy', 'gz')
- output 2: float32 [3, 256, 256], P('dp')
- output 3: float32 [3, 256], P('dp')
All inputs are finite; a program needn't handle non-finite values.
Results may differ from a plain program's by a relative error of at most 0.0125956.
Values are sent between devices in bfloat16 or wider.
A program may use at most 768 MiB of HBM per device.

v0:
```python
import jax
import jax.numpy as jnp
from jax import lax
from jax.sharding import PartitionSpec as P

PASS_FORMS = ('cayz,ai->ciyz', 'cxaz,aj->cxjz', 'cxya,ak->cxyk')


def gelu_exact(pre_act):
    return jax.nn.gelu(pre_act, approximate=False)


def band_matrix(taps, width):
    num_taps = taps.shape[0]
    offset = jnp.arange(width + num_taps - 1)[:, None] - jnp.arange(width)[None, :]
    inside = (offset >= 0) & (offset < num_taps)
    picked = taps.astype(jnp.bfloat16)[jnp.clip(offset, 0, num_taps - 1)]
    return jnp.where(inside, picked, jnp.zeros((), jnp.bfloat16))


def band_pass(padded, taps, axis):
    width = padded.shape[axis + 1] - taps.shape[0] + 1
    return jnp.einsum(PASS_FORMS[axis], padded, band_matrix(taps, width), preferred_element_type=jnp.float32)


def with_halo(block, axis_name, axis_size, axis, width):
    array_dim = axis + 1
    length = block.shape[array_dim]
    low_edge = lax.slice_in_dim(block, 0, width, axis=array_dim)
    high_edge = lax.slice_in_dim(block, length - width, length, axis=array_dim)
    if axis_size == 1:
        from_low = jnp.zeros_like(high_edge)
        from_high = jnp.zeros_like(low_edge)
    else:
        to_next = [(rank, rank + 1) for rank in range(axis_size - 1)]
        to_prev = [(rank + 1, rank) for rank in range(axis_size - 1)]
        from_low = lax.ppermute(high_edge, axis_name, to_next)
        from_high = lax.ppermute(low_edge, axis_name, to_prev)
    return jnp.concatenate([from_low, block, from_high], axis=array_dim)


def solution(mesh):
    names = ('gx', 'gy', 'gz')
    sizes = tuple(mesh.shape[axis_name] for axis_name in names)
    vol_spec = P('dp', 'gx', 'gy', 'gz')

    def local_step(volume, cot_out, filter_taps, w_mix, b_mix):
        num_layers = filter_taps.shape[0]
        half = (filter_taps.shape[2] - 1) // 2
        filtered_all = []
        pre_all = []
        vol_cur = volume
        for layer in range(num_layers):
            current = vol_cur
            for axis in range(3):
                padded = with_halo(current, names[axis], sizes[axis], axis, half)
                current = band_pass(padded, filter_taps[layer, axis], axis).astype(jnp.bfloat16)
            pre_act = jnp.einsum('cd,cxyz->dxyz', w_mix[layer], current, preferred_element_type=jnp.float32) + b_mix[layer][:, None, None, None]
            filtered_all.append(current)
            pre_all.append(pre_act)
            if layer + 1 < num_layers:
                vol_cur = (vol_cur.astype(jnp.float32) + gelu_exact(pre_act)).astype(jnp.bfloat16)
        grad_next = cot_out
        grad_w = [None] * num_layers
        grad_b = [None] * num_layers
        for layer in reversed(range(num_layers)):
            _, pullback = jax.vjp(gelu_exact, pre_all[layer])
            scaled = pullback(grad_next.astype(jnp.float32))[0]
            scaled_b = scaled.astype(jnp.bfloat16)
            grad_b[layer] = jnp.sum(scaled, axis=(1, 2, 3))
            grad_w[layer] = jnp.einsum('cxyz,dxyz->cd', filtered_all[layer], scaled_b, preferred_element_type=jnp.float32)
            current = jnp.einsum('cd,dxyz->cxyz', w_mix[layer], scaled_b, preferred_element_type=jnp.float32).astype(jnp.bfloat16)
            for axis in (2, 1, 0):
                padded = with_halo(current, names[axis], sizes[axis], axis, half)
                back = band_pass(padded, filter_taps[layer, axis][::-1], axis)
                current = back.astype(jnp.bfloat16) if axis > 0 else back
            grad_next = (grad_next.astype(jnp.float32) + current).astype(jnp.bfloat16)
        grad_w_sum = lax.psum(jnp.stack(grad_w), names)
        grad_b_sum = lax.psum(jnp.stack(grad_b), names)
        return grad_next, grad_w_sum, grad_b_sum

    return jax.shard_map(local_step, mesh=mesh, in_specs=(vol_spec, vol_spec, P(), P(), P()), out_specs=(vol_spec, P('dp'), P('dp')), check_vma=False)
```

profile of v0, /device:TPU:97, one launch (start us, length us, event | category | flops | bytes accessed | tf_op | source)
XLA Modules:
  0.0 410.9 jit_solution(4655802246182945891)
XLA Ops:
  7.3 2.8 copy.28
  11.9 4.0 collective-permute-start.1
  16.1 2.4 gather_fusion.5
  21.8 3.4 collective-permute-start.2
  26.5 2.4 gather_fusion.4
  31.1 4.3 %collective-permute-done.3 = bf16[256,16,2,16]{0,1,3,2:T(8,128)(2,1)S(1)} collective-permute-done((bf16[256,16,2,16]{0,1,3,2:T(8,128)(2,1)S(1)}, bf16[256,16,2,16]{0,1,3,2:T(8,128)(2,1)S(1)}, u32[]{:S(2)}, u32[]{:S(2)}) %collective-permute-start.3) | collective-permute-done | bytes 262176 | tf_op jit(solution)/shard_map/ppermute | solution.py:38
  35.7 3.5 convert_bitcast_fusion.10
  39.9 3.8 collective-permute-start.4
  48.8 4.5 %collective-permute-done.5 = bf16[256,16,16,2]{0,2,3,1:T(8,128)(2,1)S(1)} collective-permute-done((bf16[256,16,16,2]{0,2,3,1:T(8,128)(2,1)S(1)}, bf16[256,16,16,2]{0,2,3,1:T(8,128)(2,1)S(1)}, u32[]{:S(2)}, u32[]{:S(2)}) %collective-permute-start.5) | collective-permute-done | bytes 262176 | tf_op jit(solution)/shard_map/ppermute | solution.py:38
  54.8 11.4 %fusion.30 = (bf16[256,16,16,16]{0,3,2,1:T(8,128)(2,1)S(1)}, f32[256,16,16,16]{0,3,2,1:T(8,128)}, f32[16,16,16,256]{3,2,1,0:T(8,128)}) fusion(bf16[256,16,16,16]{0,3,2,1:T(8,128)(2,1)S(1)} %copy-done.25, f32[256]{0:T(256)S(1)} %bitcast.392, bf16[256,16,16,16]{0,3,2,1:T(8,128)(2,1)S(1)} %fusion.123, bf16[3,256,256]{2,1,0:T(8,128)(2,1)S(1)} %copy-done.34), kind=kOutput, calls=%fused_computation.74 | convolution fusion | flops 608174080 | bytes 14812160 | tf_op jit(solution)/shard_map/cd,cxyz->dxyz/dot_general | solution.py:58
  68.3 3.3 collective-permute-start.7
  71.7 2.4 gather_fusion.8
  77.3 3.3 collective-permute-start.8
  81.9 2.4 gather_fusion.7
  86.4 4.3 %collective-permute-done.9 = bf16[256,16,2,16]{0,1,3,2:T(8,128)(2,1)S(1)} collective-permute-done((bf16[256,16,2,16]{0,1,3,2:T(8,128)(2,1)S(1)}, bf16[256,16,2,16]{0,1,3,2:T(8,128)(2,1)S(1)}, u32[]{:S(2)}, u32[]{:S(2)}) %collective-permute-start.9) | collective-permute-done | bytes 262176 | tf_op jit(solution)/shard_map/ppermute | solution.py:38
  91.0 3.5 convert_bitcast_fusion.8
  95.2 3.5 collective-permute-start.10
  100.3 2.4 gather_fusion.9
  103.9 3.9 collective-permute-done.11
  109.2 11.5 %fusion.27 = (bf16[256,16,16,16]{0,3,2,1:T(8,128)(2,1)S(1)}, f32[256,16,16,16]{0,3,2,1:T(8,128)}, f32[16,16,16,256]{3,2,1,0:T(8,128)}) fusion(bf16[256,16,16,16]{0,3,2,1:T(8,128)(2,1)S(1)} %copy-done.17, f32[256]{0:T(256)S(1)} %bitcast.394, bf16[256,16,16,16]{0,3,2,1:T(8,128)(2,1)S(1)} %fusion.130, bf16[3,256,256]{2,1,0:T(8,128)(2,1)S(1)} %copy-done.34), kind=kOutput, calls=%fused_computation.66 | convolution fusion | flops 608174080 | bytes 14812160 | tf_op jit(solution)/shard_map/cd,cxyz->dxyz/dot_general | solution.py:58
  122.7 3.6 collective-permute-start.13
  131.9 3.0 collective-permute-start.14
  140.7 4.3 %collective-permute-done.15 = bf16[256,16,2,16]{0,1,3,2:T(8,128)(2,1)S(1)} collective-permute-done((bf16[256,16,2,16]{0,1,3,2:T(8,128)(2,1)S(1)}, bf16[256,16,2,16]{0,1,3,2:T(8,128)(2,1)S(1)}, u32[]{:S(2)}, u32[]{:S(2)}) %collective-permute-start.15) | collective-permute-done | bytes 262176 | tf_op jit(solution)/shard_map/ppermute | solution.py:38
  145.3 3.5 convert_bitcast_fusion.6
  149.5 3.4 collective-permute-start.16
  158.0 3.9 collective-permute-done.17
  163.3 11.9 %fusion.345 = (f32[256]{0:T(256)S(1)}, bf16[256,16,16,16]{0,3,2,1:T(8,128)(2,1)S(1)}) fusion(bf16[256,16,16,16]{0,3,2,1:T(8,128)(2,1)S(1)} %copy-done.23, f32[256]{0:T(256)S(1)} %bitcast.397, bf16[256,16,16,16]{0,3,2,1:T(8,128)(2,1)S(1)} %fusion.137, bf16[3,256,256]{2,1,0:T(8,128)(2,1)S(1)} %copy-done.34), kind=kOutput, calls=%fused_computation.382 | convolution fusion | flops 615513856 | bytes 6424576 | tf_op jit(solution)/shard_map/cd,cxyz->dxyz/dot_general | solution.py:58
  182.6 3.9 collective-permute-done.19
  186.5 2.9 fusion.152
  196.0 3.3 collective-permute-done.21
  203.0 6.2 %collective-permute-start.23 = (bf16[256,2,16,16]{0,2,3,1:T(8,128)(2,1)S(1)}, bf16[256,2,16,16]{0,2,3,1:T(8,128)(2,1)S(1)}, u32[]{:S(2)}, u32[]{:S(2)}) collective-permute-start(bf16[256,2,16,16]{0,2,3,1:T(8,128)(2,1)S(1)} %get-tuple-element.25), channel_id=1, source_target_pairs={{1,0},{3,2},{5,4},{7,6},{9,8},{11,10},{13,12},{15,14},{17,16},{19,... | collective-permute-start | bytes 786440 | tf_op jit(solution)/shard_map/ppermute | solution.py:38
  212.2 3.5 fusion.101
  215.9 3.6 fusion.321
  229.0 4.4 %collective-permute-done.25 = bf16[256,16,16,2]{0,3,2,1:T(2,128)(2,1)} collective-permute-done((bf16[256,16,16,2]{0,3,2,1:T(2,128)(2,1)S(1)}, bf16[256,16,16,2]{0,3,2,1:T(2,128)(2,1)}, u32[]{:S(2)}, u32[]{:S(2)}) %collective-permute-start.25) | collective-permute-done | bytes 262176 | tf_op jit(solution)/shard_map/ppermute | solution.py:38
  233.3 3.0 fusion.149
  244.2 3.9 collective-permute-done.27
  253.5 3.7 collective-permute-start.29
  269.6 3.5 fusion.97
  273.1 3.5 fusion.319
  282.3 3.8 collective-permute-done.30
  286.0 4.2 %collective-permute-done.31 = bf16[256,16,16,2]{0,3,2,1:T(2,128)(2,1)S(1)} collective-permute-done((bf16[256,16,16,2]{0,3,2,1:T(2,128)(2,1)S(1)}, bf16[256,16,16,2]{0,3,2,1:T(2,128)(2,1)S(1)}, u32[]{:S(2)}, u32[]{:S(2)}) %collective-permute-start.31) | collective-permute-done | bytes 262176 | tf_op jit(solution)/shard_map/ppermute | solution.py:38
  296.0 2.8 collective-permute-done.32
  298.8 3.9 collective-permute-done.33
  305.8 3.6 collective-permute-start.35
  311.1 44.0 %psum.15 = f32[3,256]{1,0:T(4,128)} all-reduce(f32[3,256]{1,0:T(4,128)S(1)} %pad_maximum_fusion.15), channel_id=1, replica_groups=mesh['dp'=1,'gz'=4,'gy'=4,'gx'=2] {'gx','gy','gz'}, use_global_device_ids=true, to_apply=%region_4.5 | all-reduce | flops 768 | bytes 6144 | tf_op jit(solution)/shard_map/psum | solution.py:79
  357.1 3.5 fusion.93
  360.6 5.9 %fusion.23 = bf16[256,16,16,16]{0,3,2,1:T(8,128)(2,1)} fusion(f32[16,256,16,16]{1,0,3,2:T(8,128)S(1)} %fusion.93, f32[16,256,16,16]{1,0,3,2:T(8,128)S(1)} %copy-done.7, bf16[256,16,16,16]{0,3,2,1:T(8,128)(2,1)S(1)} %get-tuple-element.7), kind=kLoop, calls=%fused_computation.53 | loop fusion | flops 6291456 | bytes 12582912 | tf_op jit(solution)/shard_map/convert_element_type | solution.py:77
  366.5 35.1 %all-reduce.2.cloned.1.call-done = f32[3,256,256]{2,1,0:T(8,128)} async-done(((f32[3,256,256]{2,1,0:T(8,128)}), f32[3,256,256]{2,1,0:T(8,128)}) %all-reduce.2.cloned.1.call-update) | async-done | bytes 786448 | tf_op jit(solution)/shard_map/psum | solution.py:78
  (218 shorter events, 126.9 us)
Async XLA Ops:
  7.2 8.9 %copy-start.35 = (f32[3,3,5]{2,1,0:T(4,128)S(1)}, f32[3,3,5]{2,1,0:T(4,128)}, u32[]{:S(2)}) copy-start(f32[3,3,5]{2,1,0:T(4,128)} %param.7) | copy-start | bytes 544
  7.2 394.4 %all-reduce.2.cloned.1.call-start = ((), (), s32[]{:S(2)}) async-start(), calls=%async_computation | async-start | bytes 1572864 | tf_op jit(solution)/shard_map/psum | solution.py:78
  10.6 7.9 %collective-permute-start = (bf16[256,2,16,16]{0,1,3,2:T(2,128)(2,1)S(1)}, bf16[256,2,16,16]{0,1,3,2:T(2,128)(2,1)S(1)}, u32[]{:S(2)}, u32[]{:S(2)}) collective-permute-start(bf16[256,2,16,16]{0,1,3,2:T(2,128)(2,1)S(1)} %get-tuple-element.46), channel_id=1, source_target_pairs={{0,1},{2,3},{4,5},{6,7},{8,9},{10,11},{12,13},{14,15},{16,17},{18,... | collective-permute-start | bytes 786440 | tf_op jit(solution)/shard_map/ppermute | solution.py:37
  11.9 6.6 %collective-permute-start.1 = (bf16[256,2,16,16]{0,1,3,2:T(2,128)(2,1)S(1)}, bf16[256,2,16,16]{0,1,3,2:T(2,128)(2,1)S(1)}, u32[]{:S(2)}, u32[]{:S(2)}) collective-permute-start(bf16[256,2,16,16]{0,1,3,2:T(2,128)(2,1)S(1)} %get-tuple-element.47), channel_id=1, source_target_pairs={{1,0},{3,2},{5,4},{7,6},{9,8},{11,10},{13,12},{15,14},{17,16},{19,... | collective-permute-start | bytes 786440 | tf_op jit(solution)/shard_map/ppermute | solution.py:38
  16.1 10.5 %copy-start = (bf16[5]{0:T(256)(128)(2,1)}, bf16[5]{0:T(256)(128)(2,1)S(1)}, u32[]{:S(2)}) copy-start(bf16[5]{0:T(256)(128)(2,1)S(1)} %get-tuple-element.55) | copy-start | bytes 34
  16.1 29.1 %copy-start.2 = (bf16[5]{0:T(256)(128)(2,1)}, bf16[5]{0:T(256)(128)(2,1)S(1)}, u32[]{:S(2)}) copy-start(bf16[5]{0:T(256)(128)(2,1)S(1)} %get-tuple-element.53) | copy-start | bytes 34
  21.8 13.5 %copy-start.20 = (bf16[256,16,16,16]{0,1,3,2:T(8,128)(2,1)S(1)}, bf16[256,16,16,16]{0,1,3,2:T(8,128)(2,1)}, u32[]{:S(2)}) copy-start(bf16[256,16,16,16]{0,1,3,2:T(8,128)(2,1)} %copy-done.19) | copy-start | bytes 6291460
  21.8 9.3 %collective-permute-start.2 = (bf16[256,16,2,16]{0,1,3,2:T(8,128)(2,1)S(1)}, bf16[256,16,2,16]{0,1,3,2:T(8,128)(2,1)S(1)}, u32[]{:S(2)}, u32[]{:S(2)}) collective-permute-start(bf16[256,16,2,16]{0,1,3,2:T(8,128)(2,1)S(1)} %get-tuple-element.44), channel_id=1, source_target_pairs={{0,2},{2,4},{4,6},{1,3},{3,5},{5,7},{8,10},{10,12},{12,14},{9,11},... | collective-permute-start | bytes 786440 | tf_op jit(solution)/shard_map/ppermute | solution.py:37
  25.2 10.2 %collective-permute-start.3 = (bf16[256,16,2,16]{0,1,3,2:T(8,128)(2,1)S(1)}, bf16[256,16,2,16]{0,1,3,2:T(8,128)(2,1)S(1)}, u32[]{:S(2)}, u32[]{:S(2)}) collective-permute-start(bf16[256,16,2,16]{0,1,3,2:T(8,128)(2,1)S(1)} %get-tuple-element.45), channel_id=1, source_target_pairs={{2,0},{4,2},{6,4},{3,1},{5,3},{7,5},{10,8},{12,10},{14,12},{11,9},... | collective-permute-start | bytes 786440 | tf_op jit(solution)/shard_map/ppermute | solution.py:38
  39.2 8.5 %copy-start.36 = (f32[3,256]{1,0:T(4,128)S(1)}, f32[3,256]{1,0:T(4,128)}, u32[]{:S(2)}) copy-start(f32[3,256]{1,0:T(4,128)} %param.9) | copy-start | bytes 9220
  39.9 8.9 %collective-permute-start.4 = (bf16[256,16,16,2]{0,2,3,1:T(8,128)(2,1)}, bf16[256,16,16,2]{0,2,3,1:T(8,128)(2,1)S(1)}, u32[]{:S(2)}, u32[]{:S(2)}) collective-permute-start(bf16[256,16,16,2]{0,2,3,1:T(8,128)(2,1)} %get-tuple-element.42), channel_id=1, source_target_pairs={{0,8},{8,16},{16,24},{1,9},{9,17},{17,25},{2,10},{10,18},{18,26},{... | collective-permute-start | bytes 786440 | tf_op jit(solution)/shard_map/ppermute | solution.py:37
  43.7 9.7 %collective-permute-start.5 = (bf16[256,16,16,2]{0,2,3,1:T(8,128)(2,1)S(1)}, bf16[256,16,16,2]{0,2,3,1:T(8,128)(2,1)S(1)}, u32[]{:S(2)}, u32[]{:S(2)}) collective-permute-start(bf16[256,16,16,2]{0,2,3,1:T(8,128)(2,1)S(1)} %get-tuple-element.43), channel_id=1, source_target_pairs={{8,0},{16,8},{24,16},{9,1},{17,9},{25,17},{10,2},{18,10},{26,18},{... | collective-permute-start | bytes 786440 | tf_op jit(solution)/shard_map/ppermute | solution.py:38
  54.7 11.5 %copy-start.26 = (bf16[256,16,16,16]{0,3,2,1:T(8,128)(2,1)}, bf16[256,16,16,16]{0,3,2,1:T(8,128)(2,1)S(1)}, u32[]{:S(2)}) copy-start(bf16[256,16,16,16]{0,3,2,1:T(8,128)(2,1)S(1)} %fusion.123) | copy-start | bytes 6291460
  66.2 8.0 %copy-start.16 = (bf16[256,16,16,16]{0,3,2,1:T(8,128)(2,1)}, bf16[256,16,16,16]{0,3,2,1:T(8,128)(2,1)S(1)}, u32[]{:S(2)}) copy-start(bf16[256,16,16,16]{0,3,2,1:T(8,128)(2,1)S(1)} %get-tuple-element.10) | copy-start | bytes 6291460
  67.0 7.1 %collective-permute-start.6 = (bf16[256,2,16,16]{0,3,2,1:T(8,128)(2,1)}, bf16[256,2,16,16]{0,3,2,1:T(8,128)(2,1)S(1)}, u32[]{:S(2)}, u32[]{:S(2)}) collective-permute-start(bf16[256,2,16,16]{0,3,2,1:T(8,128)(2,1)} %get-tuple-element.40), channel_id=1, source_target_pairs={{0,1},{2,3},{4,5},{6,7},{8,9},{10,11},{12,13},{14,15},{16,17},{18,... | collective-permute-start | bytes 786440 | tf_op jit(solution)/shard_map/ppermute | solution.py:37
  68.3 5.8 %collective-permute-start.7 = (bf16[256,2,16,16]{0,3,2,1:T(8,128)(2,1)S(1)}, bf16[256,2,16,16]{0,3,2,1:T(8,128)(2,1)S(1)}, u32[]{:S(2)}, u32[]{:S(2)}) collective-permute-start(bf16[256,2,16,16]{0,3,2,1:T(8,128)(2,1)S(1)} %get-tuple-element.41), channel_id=1, source_target_pairs={{1,0},{3,2},{5,4},{7,6},{9,8},{11,10},{13,12},{15,14},{17,16},{19,... | collective-permute-start | bytes 786440 | tf_op jit(solution)/shard_map/ppermute | solution.py:38
  77.3 9.2 %collective-permute-start.8 = (bf16[256,16,2,16]{0,1,3,2:T(8,128)(2,1)}, bf16[256,16,2,16]{0,1,3,2:T(8,128)(2,1)S(1)}, u32[]{:S(2)}, u32[]{:S(2)}) collective-permute-start(bf16[256,16,2,16]{0,1,3,2:T(8,128)(2,1)} %get-tuple-element.38), channel_id=1, source_target_pairs={{0,2},{2,4},{4,6},{1,3},{3,5},{5,7},{8,10},{10,12},{12,14},{9,11},... | collective-permute-start | bytes 786440 | tf_op jit(solution)/shard_map/ppermute | solution.py:37
  80.6 10.2 %collective-permute-start.9 = (bf16[256,16,2,16]{0,1,3,2:T(8,128)(2,1)S(1)}, bf16[256,16,2,16]{0,1,3,2:T(8,128)(2,1)S(1)}, u32[]{:S(2)}, u32[]{:S(2)}) collective-permute-start(bf16[256,16,2,16]{0,1,3,2:T(8,128)(2,1)S(1)} %get-tuple-element.39), channel_id=1, source_target_pairs={{2,0},{4,2},{6,4},{3,1},{5,3},{7,5},{10,8},{12,10},{14,12},{11,9},... | collective-permute-start | bytes 786440 | tf_op jit(solution)/shard_map/ppermute | solution.py:38
  95.2 8.6 %collective-permute-start.10 = (bf16[256,16,16,2]{0,2,3,1:T(8,128)(2,1)}, bf16[256,16,16,2]{0,2,3,1:T(8,128)(2,1)S(1)}, u32[]{:S(2)}, u32[]{:S(2)}) collective-permute-start(bf16[256,16,16,2]{0,2,3,1:T(8,128)(2,1)} %get-tuple-element.36), channel_id=1, source_target_pairs={{0,8},{8,16},{16,24},{1,9},{9,17},{17,25},{2,10},{10,18},{18,26},{... | collective-permute-start | bytes 786440 | tf_op jit(solution)/shard_map/ppermute | solution.py:37
  98.7 9.0 %collective-permute-start.11 = (bf16[256,16,16,2]{0,2,3,1:T(8,128)(2,1)S(1)}, bf16[256,16,16,2]{0,2,3,1:T(8,128)(2,1)S(1)}, u32[]{:S(2)}, u32[]{:S(2)}) collective-permute-start(bf16[256,16,16,2]{0,2,3,1:T(8,128)(2,1)S(1)} %get-tuple-element.37), channel_id=1, source_target_pairs={{8,0},{16,8},{24,16},{9,1},{17,9},{25,17},{10,2},{18,10},{26,18},{... | collective-permute-start | bytes 786440 | tf_op jit(solution)/shard_map/ppermute | solution.py:38
  109.1 11.5 %copy-start.28 = (bf16[256,16,16,16]{0,3,2,1:T(8,128)(2,1)}, bf16[256,16,16,16]{0,3,2,1:T(8,128)(2,1)S(1)}, u32[]{:S(2)}) copy-start(bf16[256,16,16,16]{0,3,2,1:T(8,128)(2,1)S(1)} %fusion.130) | copy-start | bytes 6291460
  121.4 7.4 %collective-permute-start.12 = (bf16[256,2,16,16]{0,3,2,1:T(8,128)(2,1)}, bf16[256,2,16,16]{0,3,2,1:T(8,128)(2,1)S(1)}, u32[]{:S(2)}, u32[]{:S(2)}) collective-permute-start(bf16[256,2,16,16]{0,3,2,1:T(8,128)(2,1)} %get-tuple-element.34), channel_id=1, source_target_pairs={{0,1},{2,3},{4,5},{6,7},{8,9},{10,11},{12,13},{14,15},{16,17},{18,... | collective-permute-start | bytes 786440 | tf_op jit(solution)/shard_map/ppermute | solution.py:37
  122.7 6.1 %collective-permute-start.13 = (bf16[256,2,16,16]{0,3,2,1:T(8,128)(2,1)S(1)}, bf16[256,2,16,16]{0,3,2,1:T(8,128)(2,1)S(1)}, u32[]{:S(2)}, u32[]{:S(2)}) collective-permute-start(bf16[256,2,16,16]{0,3,2,1:T(8,128)(2,1)S(1)} %get-tuple-element.35), channel_id=1, source_target_pairs={{1,0},{3,2},{5,4},{7,6},{9,8},{11,10},{13,12},{15,14},{17,16},{19,... | collective-permute-start | bytes 786440 | tf_op jit(solution)/shard_map/ppermute | solution.py:38
  131.9 8.9 %collective-permute-start.14 = (bf16[256,16,2,16]{0,1,3,2:T(8,128)(2,1)}, bf16[256,16,2,16]{0,1,3,2:T(8,128)(2,1)S(1)}, u32[]{:S(2)}, u32[]{:S(2)}) collective-permute-start(bf16[256,16,2,16]{0,1,3,2:T(8,128)(2,1)} %get-tuple-element.32), channel_id=1, source_target_pairs={{0,2},{2,4},{4,6},{1,3},{3,5},{5,7},{8,10},{10,12},{12,14},{9,11},... | collective-permute-start | bytes 786440 | tf_op jit(solution)/shard_map/ppermute | solution.py:37
  134.8 10.2 %collective-permute-start.15 = (bf16[256,16,2,16]{0,1,3,2:T(8,128)(2,1)S(1)}, bf16[256,16,2,16]{0,1,3,2:T(8,128)(2,1)S(1)}, u32[]{:S(2)}, u32[]{:S(2)}) collective-permute-start(bf16[256,16,2,16]{0,1,3,2:T(8,128)(2,1)S(1)} %get-tuple-element.33), channel_id=1, source_target_pairs={{2,0},{4,2},{6,4},{3,1},{5,3},{7,5},{10,8},{12,10},{14,12},{11,9},... | collective-permute-start | bytes 786440 | tf_op jit(solution)/shard_map/ppermute | solution.py:38
  149.5 8.5 %collective-permute-start.16 = (bf16[256,16,16,2]{0,2,3,1:T(8,128)(2,1)}, bf16[256,16,16,2]{0,2,3,1:T(8,128)(2,1)S(1)}, u32[]{:S(2)}, u32[]{:S(2)}) collective-permute-start(bf16[256,16,16,2]{0,2,3,1:T(8,128)(2,1)} %get-tuple-element.30), channel_id=1, source_target_pairs={{0,8},{8,16},{16,24},{1,9},{9,17},{17,25},{2,10},{10,18},{18,26},{... | collective-permute-start | bytes 786440 | tf_op jit(solution)/shard_map/ppermute | solution.py:37
  152.9 9.0 %collective-permute-start.17 = (bf16[256,16,16,2]{0,2,3,1:T(8,128)(2,1)S(1)}, bf16[256,16,16,2]{0,2,3,1:T(8,128)(2,1)S(1)}, u32[]{:S(2)}, u32[]{:S(2)}) collective-permute-start(bf16[256,16,16,2]{0,2,3,1:T(8,128)(2,1)S(1)} %get-tuple-element.31), channel_id=1, source_target_pairs={{8,0},{16,8},{24,16},{9,1},{17,9},{25,17},{10,2},{18,10},{26,18},{... | collective-permute-start | bytes 786440 | tf_op jit(solution)/shard_map/ppermute | solution.py:38
  163.3 12.0 %copy-start.30 = (bf16[256,16,16,16]{0,3,2,1:T(8,128)(2,1)}, bf16[256,16,16,16]{0,3,2,1:T(8,128)(2,1)S(1)}, u32[]{:S(2)}) copy-start(bf16[256,16,16,16]{0,3,2,1:T(8,128)(2,1)S(1)} %fusion.137) | copy-start | bytes 6291460
  176.6 5.9 %collective-permute-start.18 = (bf16[256,16,16,2]{0,3,2,1:T(2,128)(2,1)S(1)}, bf16[256,16,16,2]{0,3,2,1:T(2,128)(2,1)S(1)}, u32[]{:S(2)}, u32[]{:S(2)}) collective-permute-start(bf16[256,16,16,2]{0,3,2,1:T(2,128)(2,1)S(1)} %get-tuple-element.28), channel_id=1, source_target_pairs={{0,8},{8,16},{16,24},{1,9},{9,17},{17,25},{2,10},{10,18},{18,26},{... | collective-permute-start | bytes 786440 | tf_op jit(solution)/shard_map/ppermute | solution.py:37
  178.6 7.9 %collective-permute-start.19 = (bf16[256,16,16,2]{0,3,2,1:T(2,128)(2,1)S(1)}, bf16[256,16,16,2]{0,3,2,1:T(2,128)(2,1)S(1)}, u32[]{:S(2)}, u32[]{:S(2)}) collective-permute-start(bf16[256,16,16,2]{0,3,2,1:T(2,128)(2,1)S(1)} %get-tuple-element.29), channel_id=1, source_target_pairs={{8,0},{16,8},{24,16},{9,1},{17,9},{25,17},{10,2},{18,10},{26,18},{... | collective-permute-start | bytes 786440 | tf_op jit(solution)/shard_map/ppermute | solution.py:38
  190.1 5.9 %collective-permute-start.20 = (bf16[256,16,2,16]{0,3,2,1:T(8,128)(2,1)}, bf16[256,16,2,16]{0,3,2,1:T(8,128)(2,1)S(1)}, u32[]{:S(2)}, u32[]{:S(2)}) collective-permute-start(bf16[256,16,2,16]{0,3,2,1:T(8,128)(2,1)} %get-tuple-element.26), channel_id=1, source_target_pairs={{0,2},{2,4},{4,6},{1,3},{3,5},{5,7},{8,10},{10,12},{12,14},{9,11},... | collective-permute-start | bytes 786440 | tf_op jit(solution)/shard_map/ppermute | solution.py:37
  192.1 7.1 %collective-permute-start.21 = (bf16[256,16,2,16]{0,3,2,1:T(8,128)(2,1)S(1)}, bf16[256,16,2,16]{0,3,2,1:T(8,128)(2,1)S(1)}, u32[]{:S(2)}, u32[]{:S(2)}) collective-permute-start(bf16[256,16,2,16]{0,3,2,1:T(8,128)(2,1)S(1)} %get-tuple-element.27), channel_id=1, source_target_pairs={{2,0},{4,2},{6,4},{3,1},{5,3},{7,5},{10,8},{12,10},{14,12},{11,9},... | collective-permute-start | bytes 786440 | tf_op jit(solution)/shard_map/ppermute | solution.py:38
  201.7 10.1 %collective-permute-start.22 = (bf16[256,2,16,16]{0,2,3,1:T(8,128)(2,1)}, bf16[256,2,16,16]{0,2,3,1:T(8,128)(2,1)S(1)}, u32[]{:S(2)}, u32[]{:S(2)}) collective-permute-start(bf16[256,2,16,16]{0,2,3,1:T(8,128)(2,1)} %get-tuple-element.24), channel_id=1, source_target_pairs={{0,1},{2,3},{4,5},{6,7},{8,9},{10,11},{12,13},{14,15},{16,17},{18,... | collective-permute-start | bytes 786440 | tf_op jit(solution)/shard_map/ppermute | solution.py:37
  203.0 8.8 %collective-permute-start.23 = (bf16[256,2,16,16]{0,2,3,1:T(8,128)(2,1)S(1)}, bf16[256,2,16,16]{0,2,3,1:T(8,128)(2,1)S(1)}, u32[]{:S(2)}, u32[]{:S(2)}) collective-permute-start(bf16[256,2,16,16]{0,2,3,1:T(8,128)(2,1)S(1)} %get-tuple-element.25), channel_id=1, source_target_pairs={{1,0},{3,2},{5,4},{7,6},{9,8},{11,10},{13,12},{15,14},{17,16},{19,... | collective-permute-start | bytes 786440 | tf_op jit(solution)/shard_map/ppermute | solution.py:38
  220.9 8.1 %collective-permute-start.24 = (bf16[256,16,16,2]{0,3,2,1:T(2,128)(2,1)S(1)}, bf16[256,16,16,2]{0,3,2,1:T(2,128)(2,1)S(1)}, u32[]{:S(2)}, u32[]{:S(2)}) collective-permute-start(bf16[256,16,16,2]{0,3,2,1:T(2,128)(2,1)S(1)} %get-tuple-element.22), channel_id=1, source_target_pairs={{0,8},{8,16},{16,24},{1,9},{9,17},{17,25},{2,10},{10,18},{18,26},{... | collective-permute-start | bytes 786440 | tf_op jit(solution)/shard_map/ppermute | solution.py:37
  223.1 10.3 %collective-permute-start.25 = (bf16[256,16,16,2]{0,3,2,1:T(2,128)(2,1)S(1)}, bf16[256,16,16,2]{0,3,2,1:T(2,128)(2,1)}, u32[]{:S(2)}, u32[]{:S(2)}) collective-permute-start(bf16[256,16,16,2]{0,3,2,1:T(2,128)(2,1)S(1)} %get-tuple-element.23), channel_id=1, source_target_pairs={{8,0},{16,8},{24,16},{9,1},{17,9},{25,17},{10,2},{18,10},{26,18},{... | collective-permute-start | bytes 786440 | tf_op jit(solution)/shard_map/ppermute | solution.py:38
  237.2 6.9 %collective-permute-start.26 = (bf16[256,16,2,16]{0,3,2,1:T(8,128)(2,1)}, bf16[256,16,2,16]{0,3,2,1:T(8,128)(2,1)S(1)}, u32[]{:S(2)}, u32[]{:S(2)}) collective-permute-start(bf16[256,16,2,16]{0,3,2,1:T(8,128)(2,1)} %get-tuple-element.20), channel_id=1, source_target_pairs={{0,2},{2,4},{4,6},{1,3},{3,5},{5,7},{8,10},{10,12},{12,14},{9,11},... | collective-permute-start | bytes 786440 | tf_op jit(solution)/shard_map/ppermute | solution.py:37
  238.9 9.1 %collective-permute-start.27 = (bf16[256,16,2,16]{0,3,2,1:T(8,128)(2,1)S(1)}, bf16[256,16,2,16]{0,3,2,1:T(8,128)(2,1)S(1)}, u32[]{:S(2)}, u32[]{:S(2)}) collective-permute-start(bf16[256,16,2,16]{0,3,2,1:T(8,128)(2,1)S(1)} %get-tuple-element.21), channel_id=1, source_target_pairs={{2,0},{4,2},{6,4},{3,1},{5,3},{7,5},{10,8},{12,10},{14,12},{11,9},... | collective-permute-start | bytes 786440 | tf_op jit(solution)/shard_map/ppermute | solution.py:38
  252.2 15.3 %collective-permute-start.28 = (bf16[256,2,16,16]{0,2,3,1:T(8,128)(2,1)}, bf16[256,2,16,16]{0,2,3,1:T(8,128)(2,1)S(1)}, u32[]{:S(2)}, u32[]{:S(2)}) collective-permute-start(bf16[256,2,16,16]{0,2,3,1:T(8,128)(2,1)} %get-tuple-element.18), channel_id=1, source_target_pairs={{0,1},{2,3},{4,5},{6,7},{8,9},{10,11},{12,13},{14,15},{16,17},{18,... | collective-permute-start | bytes 786440 | tf_op jit(solution)/shard_map/ppermute | solution.py:37
  253.5 14.0 %collective-permute-start.29 = (bf16[256,2,16,16]{0,2,3,1:T(8,128)(2,1)S(1)}, bf16[256,2,16,16]{0,2,3,1:T(8,128)(2,1)S(1)}, u32[]{:S(2)}, u32[]{:S(2)}) collective-permute-start(bf16[256,2,16,16]{0,2,3,1:T(8,128)(2,1)S(1)} %get-tuple-element.19), channel_id=1, source_target_pairs={{1,0},{3,2},{5,4},{7,6},{9,8},{11,10},{13,12},{15,14},{17,16},{19,... | collective-permute-start | bytes 786440 | tf_op jit(solution)/shard_map/ppermute | solution.py:38
  278.0 8.1 %collective-permute-start.30 = (bf16[256,16,16,2]{0,3,2,1:T(2,128)(2,1)S(1)}, bf16[256,16,16,2]{0,3,2,1:T(2,128)(2,1)S(1)}, u32[]{:S(2)}, u32[]{:S(2)}) collective-permute-start(bf16[256,16,16,2]{0,3,2,1:T(2,128)(2,1)S(1)} %get-tuple-element.16), channel_id=1, source_target_pairs={{0,8},{8,16},{16,24},{1,9},{9,17},{17,25},{2,10},{10,18},{18,26},{... | collective-permute-start | bytes 786440 | tf_op jit(solution)/shard_map/ppermute | solution.py:37
  280.1 10.1 %collective-permute-start.31 = (bf16[256,16,16,2]{0,3,2,1:T(2,128)(2,1)S(1)}, bf16[256,16,16,2]{0,3,2,1:T(2,128)(2,1)S(1)}, u32[]{:S(2)}, u32[]{:S(2)}) collective-permute-start(bf16[256,16,16,2]{0,3,2,1:T(2,128)(2,1)S(1)} %get-tuple-element.17), channel_id=1, source_target_pairs={{8,0},{16,8},{24,16},{9,1},{17,9},{25,17},{10,2},{18,10},{26,18},{... | collective-permute-start | bytes 786440 | tf_op jit(solution)/shard_map/ppermute | solution.py:38
  282.2 13.0 %copy-start.11 = (bf16[256,16,16,16]{0,3,2,1:T(8,128)(2,1)S(1)}, bf16[256,16,16,16]{0,3,2,1:T(8,128)(2,1)}, u32[]{:S(2)}) copy-start(bf16[256,16,16,16]{0,3,2,1:T(8,128)(2,1)} %copy-done.10) | copy-start | bytes 6291460
  282.3 13.0 %copy-start.29 = (bf16[256,16,16,16]{0,3,2,1:T(8,128)(2,1)S(1)}, bf16[256,16,16,16]{0,3,2,1:T(8,128)(2,1)}, u32[]{:S(2)}) copy-start(bf16[256,16,16,16]{0,3,2,1:T(8,128)(2,1)} %copy-done.28) | copy-start | bytes 6291460
  291.7 7.1 %collective-permute-start.32 = (bf16[256,16,2,16]{0,3,2,1:T(8,128)(2,1)S(1)}, bf16[256,16,2,16]{0,3,2,1:T(8,128)(2,1)S(1)}, u32[]{:S(2)}, u32[]{:S(2)}) collective-permute-start(bf16[256,16,2,16]{0,3,2,1:T(8,128)(2,1)S(1)} %get-tuple-element.14), channel_id=1, source_target_pairs={{0,2},{2,4},{4,6},{1,3},{3,5},{5,7},{8,10},{10,12},{12,14},{9,11},... | collective-permute-start | bytes 786440 | tf_op jit(solution)/shard_map/ppermute | solution.py:37
  293.7 9.0 %collective-permute-start.33 = (bf16[256,16,2,16]{0,3,2,1:T(8,128)(2,1)S(1)}, bf16[256,16,2,16]{0,3,2,1:T(8,128)(2,1)S(1)}, u32[]{:S(2)}, u32[]{:S(2)}) collective-permute-start(bf16[256,16,2,16]{0,3,2,1:T(8,128)(2,1)S(1)} %get-tuple-element.15), channel_id=1, source_target_pairs={{2,0},{4,2},{6,4},{3,1},{5,3},{7,5},{10,8},{12,10},{14,12},{11,9},... | collective-permute-start | bytes 786440 | tf_op jit(solution)/shard_map/ppermute | solution.py:38
  304.4 50.7 %collective-permute-start.34 = (bf16[256,2,16,16]{0,2,3,1:T(8,128)(2,1)S(1)}, bf16[256,2,16,16]{0,2,3,1:T(8,128)(2,1)S(1)}, u32[]{:S(2)}, u32[]{:S(2)}) collective-permute-start(bf16[256,2,16,16]{0,2,3,1:T(8,128)(2,1)S(1)} %get-tuple-element.12), channel_id=1, source_target_pairs={{0,1},{2,3},{4,5},{6,7},{8,9},{10,11},{12,13},{14,15},{16,17},{18,... | collective-permute-start | bytes 786440 | tf_op jit(solution)/shard_map/ppermute | solution.py:37
  305.8 49.4 %collective-permute-start.35 = (bf16[256,2,16,16]{0,2,3,1:T(8,128)(2,1)S(1)}, bf16[256,2,16,16]{0,2,3,1:T(8,128)(2,1)S(1)}, u32[]{:S(2)}, u32[]{:S(2)}) collective-permute-start(bf16[256,2,16,16]{0,2,3,1:T(8,128)(2,1)S(1)} %get-tuple-element.13), channel_id=1, source_target_pairs={{1,0},{3,2},{5,4},{7,6},{9,8},{11,10},{13,12},{15,14},{17,16},{19,... | collective-permute-start | bytes 786440 | tf_op jit(solution)/shard_map/ppermute | solution.py:38
  (26 other events, 131.2 us)
Sparse Core Ops, SparseCore 0:
  311.2 90.2 all-reduce.1
where the time goes:
time: 419 us; the launch traced here: 411 us
  waiting for transfers between devices  103 us (25%)
  starting transfers between devices  81.2 us (19%)
  matrix products  80.7 us (19%)
  local copies, waits for them, and re-layouts  62.5 us (15%)
  blocking collectives  44 us (11%)
  other arithmetic  23.4 us (6%)
  between operations  15.7 us (4%)
    ppermute x18, waiting for transfers between devices, with_halo(): from_high = lax.ppermute(low_edge, axis_name, to_prev)  48.7 us
    gather x36, local copies, waits for them, and re-layouts, band_matrix(): picked = taps.astype(jnp.bfloat16)[jnp.clip(offset, 0, num_taps - 1)]  44.1 us
    psum x1, blocking collectives, local_step(): grad_b_sum = lax.psum(jnp.stack(grad_b), names)  44 us
    dot_general x18, matrix products, band_pass(): jnp.einsum(PASS_FORMS[axis], padded, band_matrix(taps, width), preferred_...  41.4 us
    ppermute x18, starting transfers between devices, with_halo(): from_high = lax.ppermute(low_edge, axis_name, to_prev)  41.1 us
    ppermute x18, starting transfers between devices, with_halo(): from_low = lax.ppermute(high_edge, axis_name, to_next)  40 us
    psum x1, waiting for transfers between devices, local_step(): grad_w_sum = lax.psum(jnp.stack(grad_w), names)  35.1 us
    dot_general x3, matrix products, local_step(): jnp.einsum('cd,cxyz->dxyz', w_mix[layer], current, preferred_element_type...  34.8 us
  transfers between devices with their start and end apart: 37, of which 24 were waited for; matrix products, arithmetic and copies ran while one was open for 15% of the time, Pallas kernels for 0%

commit v1 on v0

v1 whole, which is shorter than its diff:
```python
import functools

import jax
import jax.numpy as jnp
from jax import lax
from jax.experimental import pallas as pl
from jax.experimental.pallas import tpu as pltpu
from jax.sharding import PartitionSpec as P

MESH = pl.DeviceIdType.MESH
PLANES = 2
LAG = 1
XLAG = 1
F32 = jnp.float32
BF16 = jnp.bfloat16
SQRT_HALF = 0.7071067811865476
INV_SQRT_2PI = 0.3989422804014327


def dot(a, b):
    return jnp.dot(a, b, preferred_element_type=F32)


def stage_list(num_layers):
    stages = []
    start = 0
    for layer in range(num_layers):
        stages.append(('fx', layer, start))
        stages.append(('fy', layer, start + LAG))
        stages.append(('fz', layer, start + 2 * LAG))
        start += 2 * LAG + (XLAG if layer + 1 < num_layers else 0)
    for layer in reversed(range(num_layers)):
        stages.append(('bs', layer, start))
        stages.append(('bz', layer, start + LAG))
        stages.append(('by', layer, start + 2 * LAG))
        stages.append(('bx', layer, start + 2 * LAG + XLAG))
        start += 2 * LAG + XLAG
    return stages, start


def kernel(sizes, vol, cot, taps, w, b, out, gw_out, gb_out,
           vols, a1, a2, a3, gp, grad, d3, d2, d1, sb, yh, zh, zs, gb_acc,
           mfy, mfyh, mfz, mfzh, mby, mbyh, mbz, mbzh, sel,
           in_sem, cot_sem, out_sem, ysend, yrecv, zsend, zrecv, xsend, xrecv):
    nx, ny, nz, num_layers, num_taps, by_len, bz_len = sizes
    half = (num_taps - 1) // 2
    planes = a1.shape[0]
    rows = by_len * bz_len
    edge_y = half * bz_len
    edge_z = half * by_len
    nt = planes // PLANES
    my_x, my_y, my_z = lax.axis_index('gx'), lax.axis_index('gy'), lax.axis_index('gz')
    y_lo, y_hi = my_y > 0, my_y < ny - 1
    z_lo, z_hi = my_z > 0, my_z < nz - 1
    y_prev, y_next = {'gy': jnp.maximum(my_y - 1, 0)}, {'gy': jnp.minimum(my_y + 1, ny - 1)}
    z_prev, z_next = {'gz': jnp.maximum(my_z - 1, 0)}, {'gz': jnp.minimum(my_z + 1, nz - 1)}
    x_peer = {'gx': 1 - my_x}

    def x_of(j):
        return my_x * j + (1 - my_x) * (planes - 1 - j)

    def in_copy(j):
        return pltpu.make_async_copy(vol.at[x_of(j)], vols.at[0, j + half], in_sem.at[j])

    def cot_copy(j):
        return pltpu.make_async_copy(cot.at[x_of(j)], grad.at[j], cot_sem.at[j])

    def start_in(j, carry):
        in_copy(j).start()
        cot_copy(j).start()
        return carry

    lax.fori_loop(0, planes, start_in, 0)

    barrier = pltpu.get_barrier_semaphore()
    pl.semaphore_signal(barrier, inc=1, device_id=x_peer, device_id_type=MESH)
    for has, device in ((y_lo, y_prev), (y_hi, y_next), (z_lo, z_prev), (z_hi, z_next)):
        @pl.when(has)
        def _():
            pl.semaphore_signal(barrier, inc=1, device_id=device, device_id_type=MESH)

    def iota(shape, axis):
        return lax.broadcasted_iota(jnp.int32, shape, axis)

    def banded(layer, axis, back, diff, step, inside):
        total = jnp.zeros(diff.shape, F32)
        for t in range(num_taps):
            tap = taps[(layer * 3 + axis) * num_taps + (num_taps - 1 - t if back else t)]
            total = jnp.where(diff == step * (t - half), tap, total)
        if inside is not None:
            total = jnp.where(inside, total, 0.0)
        return total.astype(BF16)

    def build_chunk(chunk, carry):
        size = 64
        base = pl.multiple_of(chunk * size, size)
        at = pl.ds(base, size)
        halo_cols = 2 * edge_y
        i_in, k_in = base + iota((size, rows), 0), iota((size, rows), 1)
        i_halo, k_halo = base + iota((size, halo_cols), 0), iota((size, halo_cols), 1)
        k_y = jnp.where(k_halo < edge_y, k_halo - edge_y, k_halo + rows - edge_y)
        side = k_halo // edge_z
        hop = (k_halo % edge_z) // by_len
        zin = jnp.where(side == 0, hop - half, hop + bz_len)
        same_y = k_halo % by_len == i_halo // bz_len
        same_row = k_in // bz_len == i_in // bz_len
        for layer in range(num_layers):
            mfy[layer, at, :] = banded(layer, 1, False, k_in - i_in, bz_len, None)
            mby[layer, at, :] = banded(layer, 1, True, k_in - i_in, bz_len, None)
            mfyh[layer, at, :] = banded(layer, 1, False, k_y - i_halo, bz_len, None)
            mbyh[layer, at, :] = banded(layer, 1, True, k_y - i_halo, bz_len, None)
            mfz[layer, at, :] = banded(layer, 2, False, k_in - i_in, 1, same_row)
            mbz[layer, at, :] = banded(layer, 2, True, k_in - i_in, 1, same_row)
            mfzh[layer, at, :] = banded(layer, 2, False, zin - i_halo % bz_len, 1, same_y)
            mbzh[layer, at, :] = banded(layer, 2, True, zin - i_halo % bz_len, 1, same_y)
        return carry

    lax.fori_loop(0, rows // 64, build_chunk, 0)
    q, k_in = iota((2 * edge_z, rows), 0), iota((2 * edge_z, rows), 1)
    i_edge = (q % by_len) * bz_len + (q % edge_z) // by_len + (q // edge_z) * (bz_len - half)
    sel[...] = jnp.where(k_in == i_edge, 1.0, 0.0).astype(BF16)
    q, k_halo = iota((2 * edge_z, 2 * edge_y), 0), iota((2 * edge_z, 2 * edge_y), 1)
    i_edge_h = (q % by_len) * bz_len + (q % edge_z) // by_len + (q // edge_z) * (bz_len - half)
    k_y = jnp.where(k_halo < edge_y, k_halo - edge_y, k_halo + rows - edge_y)
    for layer in range(num_layers):
        mfy[layer, rows:, :] = banded(layer, 1, False, k_in - i_edge, bz_len, None)
        mfyh[layer, rows:, :] = banded(layer, 1, False, k_y - i_edge_h, bz_len, None)

    for layer in range(num_layers):
        vols[layer, planes + half:] = jnp.zeros((half,) + vols.shape[2:], BF16)
        d1[layer, planes + half:] = jnp.zeros((half,) + d1.shape[2:], BF16)

    def zero_halo(halo, where, side, edge):
        @pl.when(where)
        def _():
            def clear(j, carry):
                for stage in range(2 * num_layers):
                    halo[stage, j, side * edge:(side + 1) * edge] = jnp.zeros((edge, halo.shape[3]), BF16)
                return carry
            lax.fori_loop(0, planes, clear, 0)

    zero_halo(yh, my_y == 0, 0, edge_y)
    zero_halo(yh, my_y == ny - 1, 1, edge_y)
    zero_halo(zh, my_z == 0, 0, edge_z)
    zero_halo(zh, my_z == nz - 1, 1, edge_z)
    gw_out[...] = jnp.zeros(gw_out.shape, F32)
    gb_acc[...] = jnp.zeros(gb_acc.shape, F32)

    pl.semaphore_wait(barrier, 1 + y_lo.astype(jnp.int32) + y_hi.astype(jnp.int32) + z_lo.astype(jnp.int32) + z_hi.astype(jnp.int32))

    def y_copies(src, stage, tau):
        at = pl.ds(tau * PLANES, PLANES)
        up = pltpu.make_async_remote_copy(
            src_ref=src.at[at, pl.ds(rows - edge_y, edge_y)], dst_ref=yh.at[stage, at, pl.ds(0, edge_y)],
            send_sem=ysend.at[stage, tau, 0], recv_sem=yrecv.at[stage, tau, 0], device_id=y_next, device_id_type=MESH)
        dn = pltpu.make_async_remote_copy(
            src_ref=src.at[at, pl.ds(0, edge_y)], dst_ref=yh.at[stage, at, pl.ds(edge_y, edge_y)],
            send_sem=ysend.at[stage, tau, 1], recv_sem=yrecv.at[stage, tau, 1], device_id=y_prev, device_id_type=MESH)
        return up, dn, y_lo, y_hi

    def z_copies(stage, tau):
        at = pl.ds(tau * PLANES, PLANES)
        up = pltpu.make_async_remote_copy(
            src_ref=zs.at[stage, at, pl.ds(edge_z, edge_z)], dst_ref=zh.at[stage, at, pl.ds(0, edge_z)],
            send_sem=zsend.at[stage, tau, 0], recv_sem=zrecv.at[stage, tau, 0], device_id=z_next, device_id_type=MESH)
        dn = pltpu.make_async_remote_copy(
            src_ref=zs.at[stage, at, pl.ds(0, edge_z)], dst_ref=zh.at[stage, at, pl.ds(edge_z, edge_z)],
            send_sem=zsend.at[stage, tau, 1], recv_sem=zrecv.at[stage, tau, 1], device_id=z_prev, device_id_type=MESH)
        return up, dn, z_lo, z_hi

    def start(copies):
        up, dn, has_lo, has_hi = copies
        pl.when(has_hi)(up.start)
        pl.when(has_lo)(dn.start)

    def wait(copies):
        up, dn, has_lo, has_hi = copies

        @pl.when(has_hi)
        def _():
            up.wait_send()
            dn.wait_recv()

        @pl.when(has_lo)
        def _():
            dn.wait_send()
            up.wait_recv()

    def x_copy(buf, stage, layer, j):
        src = vol.at[x_of(j)] if stage == 0 else buf.at[layer, half + j]
        return pltpu.make_async_remote_copy(
            src_ref=src, dst_ref=buf.at[layer, half - 1 - j],
            send_sem=xsend.at[stage, j], recv_sem=xrecv.at[stage, j], device_id=x_peer, device_id_type=MESH)

    def start_x(buf, stage, layer, tau):
        for task in range(-(-half // PLANES)):
            @pl.when(tau == task)
            def _():
                for j in range(task * PLANES, min(half, (task + 1) * PLANES)):
                    x_copy(buf, stage, layer, j).start()

    def wait_x(buf, stage, layer, tau):
        @pl.when(tau == 0)
        def _():
            for j in range(half):
                x_copy(buf, stage, layer, j).wait()

    for j in range(half):
        x_copy(vols, 0, 0, j).start()

    def wait_in(j, carry):
        in_copy(j).wait()
        return carry

    lax.fori_loop(0, planes, wait_in, 0)

    def x_tap(layer, back, u):
        base = layer * 3 * num_taps
        plain, flipped = taps[base + u], taps[base + num_taps - 1 - u]
        return jnp.where(my_x == 1, flipped, plain) if back else jnp.where(my_x == 1, plain, flipped)

    def x_pass(buf, layer, back, tau, emit):
        weights = [x_tap(layer, back, u) for u in range(num_taps)]
        size = 16

        def body(chunk, carry):
            at = pl.ds(pl.multiple_of(chunk * size, size), size)
            loaded = [buf[layer, tau * PLANES + p, at, :].astype(F32) for p in range(PLANES + num_taps - 1)]
            for p in range(PLANES):
                total = weights[0] * loaded[p]
                for u in range(1, num_taps):
                    total = total + weights[u] * loaded[p + u]
                emit(tau * PLANES + p, at, total)
            return carry

        lax.fori_loop(0, rows // size, body, 0, unroll=2)

    def fx(layer, tau):
        wait_x(vols, layer, layer, tau)

        def emit(j, at, total):
            a1[j, at, :] = total.astype(BF16)

        x_pass(vols, layer, False, tau, emit)
        start(y_copies(a1, layer, tau))

    def fy(layer, tau):
        wait(y_copies(a1, layer, tau))
        for p in range(PLANES):
            j = tau * PLANES + p
            total = dot(mfy[layer], a1[j]) + dot(mfyh[layer], yh[layer, j])
            a2[j] = total[:rows].astype(BF16)
            zs[layer, j] = total[rows:].astype(BF16)
        start(z_copies(layer, tau))

    def fz(layer, tau):
        wait(z_copies(layer, tau))
        for p in range(PLANES):
            j = tau * PLANES + p
            total = dot(mfz[layer], a2[j]) + dot(mfzh[layer], zh[layer, j])
            filtered = total.astype(BF16)
            a3[layer, j] = filtered
            gp[layer, j] = dot(filtered, w[layer]) + b[layer, :][None, :]
        size = 16

        def body(chunk, carry):
            at = pl.ds(pl.multiple_of(chunk * size, size), size)
            for p in range(PLANES):
                j = tau * PLANES + p
                z = gp[layer, j, at, :]
                cdf = 0.5 * (1.0 + lax.erf(z * SQRT_HALF))
                gp[layer, j, at, :] = cdf + z * (jnp.exp(-0.5 * (z * z)) * INV_SQRT_2PI)
                if layer + 1 < num_layers:
                    vols[layer + 1, j + half, at, :] = (vols[layer, j + half, at, :].astype(F32) + z * cdf).astype(BF16)
            return carry

        lax.fori_loop(0, rows // size, body, 0, unroll=2)
        if layer + 1 < num_layers:
            start_x(vols, layer + 1, layer + 1, tau)

    def bs(layer, tau):
        stage = num_layers + layer
        if layer == num_layers - 1:
            for p in range(PLANES):
                cot_copy(tau * PLANES + p).wait()
        size = 16

        def body(chunk, acc):
            at = pl.ds(pl.multiple_of(chunk * size, size), size)
            for p in range(PLANES):
                j = tau * PLANES + p
                scaled = gp[layer, j, at, :] * grad[j, at, :].astype(F32)
                sb[p, at, :] = scaled.astype(BF16)
                acc = acc + scaled[:8] + scaled[8:]
            return acc

        gb_acc[layer] = lax.fori_loop(0, rows // size, body, gb_acc[layer], unroll=2)
        for p in range(PLANES):
            j = tau * PLANES + p
            mixed = lax.dot_general(sb[p], w[layer], (((1,), (1,)), ((), ())), preferred_element_type=F32).astype(BF16)
            d3[j] = mixed
            zs[stage, j] = dot(sel[...], mixed).astype(BF16)
        start(z_copies(stage, tau))
        for p in range(PLANES):
            j = tau * PLANES + p
            gw_out[layer] += lax.dot_general(a3[layer, j], sb[p], (((0,), (0,)), ((), ())), preferred_element_type=F32)

    def bz(layer, tau):
        stage = num_layers + layer
        wait(z_copies(stage, tau))
        for p in range(PLANES):
            j = tau * PLANES + p
            d2[j] = (dot(mbz[layer], d3[j]) + dot(mbzh[layer], zh[stage, j])).astype(BF16)
        start(y_copies(d2, stage, tau))

    def by(layer, tau):
        stage = num_layers + layer
        wait(y_copies(d2, stage, tau))
        for p in range(PLANES):
            j = tau * PLANES + p
            d1[layer, j + half] = (dot(mby[layer], d2[j]) + dot(mbyh[layer], yh[stage, j])).astype(BF16)
        start_x(d1, stage, layer, tau)

    def out_copy(j):
        return pltpu.make_async_copy(grad.at[j], out.at[x_of(j)], out_sem.at[j])

    def bx(layer, tau):
        wait_x(d1, num_layers + layer, layer, tau)

        def emit(j, at, total):
            grad[j, at, :] = (grad[j, at, :].astype(F32) + total).astype(BF16)

        x_pass(d1, layer, True, tau, emit)
        if layer == 0:
            for p in range(PLANES):
                out_copy(tau * PLANES + p).start()

    tasks = {'fx': fx, 'fy': fy, 'fz': fz, 'bs': bs, 'bz': bz, 'by': by, 'bx': bx}
    stages, last = stage_list(num_layers)

    def step(s, carry):
        for kind, layer, first in stages:
            tau = s - first

            @pl.when((tau >= 0) & (tau < nt))
            def _():
                tasks[kind](layer, tau)
        return carry

    lax.fori_loop(0, last + nt, step, 0)
    gb_out[...] = jnp.sum(gb_acc[...], axis=1)

    def wait_out(j, carry):
        out_copy(j).wait()
        return carry

    lax.fori_loop(0, planes, wait_out, 0)


def solution(mesh):
    names = ('gx', 'gy', 'gz')
    nx, ny, nz = (mesh.shape[axis_name] for axis_name in names)
    assert nx == 2
    vol_spec = P('dp', 'gx', 'gy', 'gz')

    def local_step(volume, cot_out, filter_taps, w_mix, b_mix):
        channels, planes, by_len, bz_len = volume.shape
        num_layers, _, num_taps = filter_taps.shape
        half = (num_taps - 1) // 2
        rows = by_len * bz_len
        edge_y, edge_z = half * bz_len, half * by_len
        nt = planes // PLANES
        stages = 2 * num_layers

        def to_rows(block):
            return jnp.transpose(block, (1, 2, 3, 0)).reshape(planes, rows, channels)

        any_spec = pl.BlockSpec(memory_space=pl.ANY)
        vmem_spec = pl.BlockSpec(memory_space=pltpu.VMEM)
        smem_spec = pl.BlockSpec(memory_space=pltpu.SMEM)
        block = (planes, rows, channels)
        dma = pltpu.SemaphoreType.DMA
        grad_rows, grad_w, grad_b = pl.pallas_call(
            functools.partial(kernel, (nx, ny, nz, num_layers, num_taps, by_len, bz_len)),
            out_shape=(
                jax.ShapeDtypeStruct(block, BF16),
                jax.ShapeDtypeStruct((num_layers, channels, channels), F32),
                jax.ShapeDtypeStruct((num_layers, channels), F32),
            ),
            in_specs=[any_spec, any_spec, smem_spec, vmem_spec, vmem_spec],
            out_specs=(any_spec, vmem_spec, vmem_spec),
            scratch_shapes=[
                pltpu.VMEM((num_layers, planes + 2 * half, rows, channels), BF16),
                pltpu.VMEM(block, BF16),
                pltpu.VMEM(block, BF16),
                pltpu.VMEM((num_layers,) + block, BF16),
                pltpu.VMEM((num_layers,) + block, F32),
                pltpu.VMEM(block, BF16),
                pltpu.VMEM(block, BF16),
                pltpu.VMEM(block, BF16),
                pltpu.VMEM((num_layers, planes + 2 * half, rows, channels), BF16),
                pltpu.VMEM((PLANES, rows, channels), BF16),
                pltpu.VMEM((stages, planes, 2 * edge_y, channels), BF16),
                pltpu.VMEM((stages, planes, 2 * edge_z, channels), BF16),
                pltpu.VMEM((stages, planes, 2 * edge_z, channels), BF16),
                pltpu.VMEM((num_layers, 8, channels), F32),
                pltpu.VMEM((num_layers, rows + 2 * edge_z, rows), BF16),
                pltpu.VMEM((num_layers, rows + 2 * edge_z, 2 * edge_y), BF16),
                pltpu.VMEM((num_layers, rows, rows), BF16),
                pltpu.VMEM((num_layers, rows, 2 * edge_z), BF16),
                pltpu.VMEM((num_layers, rows, rows), BF16),
                pltpu.VMEM((num_layers, rows, 2 * edge_y), BF16),
                pltpu.VMEM((num_layers, rows, rows), BF16),
                pltpu.VMEM((num_layers, rows, 2 * edge_z), BF16),
                pltpu.VMEM((2 * edge_z, rows), BF16),
                dma((planes,)), dma((planes,)), dma((planes,)),
                dma((stages, nt, 2)), dma((stages, nt, 2)), dma((stages, nt, 2)), dma((stages, nt, 2)),
                dma((stages, half)), dma((stages, half)),
            ],
            compiler_params=pltpu.CompilerParams(
                collective_id=0, has_side_effects=True, vmem_limit_bytes=64000 * 1024),
            name='stack',
        )(to_rows(volume), to_rows(cot_out), filter_taps.reshape(-1), w_mix, b_mix)
        grad_volume = jnp.transpose(grad_rows.reshape(planes, by_len, bz_len, channels), (3, 0, 1, 2))
        grad_w_sum = lax.psum(grad_w, names)
        grad_b_sum = lax.psum(grad_b, names)
        return grad_volume, grad_w_sum, grad_b_sum

    return jax.shard_map(local_step, mesh=mesh, in_specs=(vol_spec, vol_spec, P(), P(), P()), out_specs=(vol_spec, P('dp'), P('dp')), check_vma=False)
```

time: 419 us -> 230 us (0.55); the launches traced: 411 us -> 229 us
  Pallas kernels: 0 us -> 112 us
  starting transfers between devices: 81.2 us -> 0.06 us
  matrix products: 80.7 us -> 0 us
  local copies, waits for them, and re-layouts: 62.5 us -> 5.34 us
  waiting for transfers between devices: 103 us -> 50.9 us
  other arithmetic: 23.4 us -> 0 us
    pallas_call x0 -> x1, Pallas kernels: none -> 112 us  [local_step(): pl.pallas_call(functools.partial(kernel, (nx, ny, nz, num_layers, num_tap...]
    ppermute x36 -> x0, starting transfers between devices: 81.1 us -> none  [the longest x18 41.1 us: with_halo(): from_high = lax.ppermute(low_edge, axis_name, to_prev)]
    dot_general x27 -> x0, matrix products: 80.7 us -> none  [the longest x18 41.4 us: band_pass(): jnp.einsum(PASS_FORMS[axis], padded, band_matrix(taps, width), preferred_...]
    ppermute x36 -> x0, waiting for transfers between devices: 68.3 us -> none  [the longest x18 48.7 us: with_halo(): from_high = lax.ppermute(low_edge, axis_name, to_prev)]
    gather x36 -> x0, local copies, waits for them, and re-layouts: 44.1 us -> none  [band_matrix(): picked = taps.astype(jnp.bfloat16)[jnp.clip(offset, 0, num_taps - 1)]]
    psum x1, waiting for transfers between devices: 35.1 us -> 50.8 us  [local_step(): grad_w_sum = lax.psum(grad_w, names)]
    slice x19 -> x0, local copies, waits for them, and re-layouts: 10.9 us -> none  [the longest x18 10.9 us: with_halo(): high_edge = lax.slice_in_dim(block, length - width, length, axis=array_dim)]
    concatenate x14 -> x0, other arithmetic: 9.45 us -> none  [with_halo(): return jnp.concatenate([from_low, block, from_high], axis=array_dim)]
  transfers between devices with their start and end apart: 37 -> 1, of which waited for: 24 -> 1; matrix products, arithmetic and copies ran while one was open for 15% -> 0% of each run, Pallas kernels for 0% -> 0%
where the time goes in v1:
time: 230 us; the launch traced here: 229 us
  Pallas kernels  112 us (49%)
  waiting for transfers between devices  50.9 us (22%)
  blocking collectives  46.7 us (20%)
  between operations  14.1 us (6%)
  local copies, waits for them, and re-layouts  5.34 us (2%)
    pallas_call x1, Pallas kernels, local_step(): pl.pallas_call(functools.partial(kernel, (nx, ny, nz, num_layers, num_tap...  112 us
    psum x1, waiting for transfers between devices, local_step(): grad_w_sum = lax.psum(grad_w, names)  50.8 us
    psum x1, blocking collectives, local_step(): grad_b_sum = lax.psum(grad_b, names)  46.7 us
  transfers between devices with their start and end apart: 1, of which 1 were waited for; matrix products, arithmetic and copies ran while one was open for 0% of the time, Pallas kernels for 0%

profile of v1, /device:TPU:97, one launch (start us, length us, event | category | flops | bytes accessed | tf_op | source)
XLA Modules:
  0.0 229.2 jit_solution(3381633079088240493)
XLA Ops:
  7.2 0.1 all-reduce.2.cloned.1.call-start
  7.2 1.3 reshape.20.taps
  8.5 112.2 %stack.1 = (bf16[16,256,256]{2,1,0:T(8,128)(2,1)}, f32[3,256,256]{2,1,0:T(8,128)}, f32[3,256]{1,0:T(4,128)}) custom-call(bf16[16,256,256]{2,1,0:T(8,128)(2,1)} %bitcast.9, bf16[16,256,256]{2,1,0:T(8,128)(2,1)} %bitcast.10, f32[45]{0:T(128)} %reshape.20.taps, bf16[3,256,256]{2,1,0:T(8,128)(2,1)} %w.1, f32[3,256]{1,0:T(4,128)} %b.1), custom_call_target="tpu_custom_call" | custom-call | tf_op jit(solution)/shard_map/stack/pallas_call | solution.py:383
  120.7 0.1 all-reduce.2.cloned.1.call-update
  120.8 46.7 %psum.15 = f32[3,256]{1,0:T(4,128)} all-reduce(f32[3,256]{1,0:T(4,128)} %get-tuple-element.8), channel_id=1, replica_groups=mesh['dp'=1,'gz'=4,'gy'=4,'gx'=2] {'gx','gy','gz'}, use_global_device_ids=true, to_apply=%region_1.0 | all-reduce | flops 768 | bytes 6144 | tf_op jit(solution)/shard_map/psum | solution.py:426
  167.5 50.8 %all-reduce.2.cloned.1.call-done = f32[3,256,256]{2,1,0:T(8,128)} async-done(((f32[3,256,256]{2,1,0:T(8,128)}), f32[3,256,256]{2,1,0:T(8,128)}) %all-reduce.2.cloned.1.call-update) | async-done | bytes 786448 | tf_op jit(solution)/shard_map/psum | solution.py:425
  218.3 0.0 copy-start
  218.3 3.2 %copy.11 = bf16[256,16,16,16]{0,3,2,1:T(8,128)(2,1)} copy(bf16[256,16,16,16]{0,3,2,1:T(8,128)(2,1)} %bitcast.11) | data formatting | bytes 4194304
  221.5 0.0 copy-done
  221.5 0.9 copy.12
Async XLA Ops:
  7.2 211.1 %all-reduce.2.cloned.1.call-start = ((), (), s32[]{:S(2)}) async-start(), calls=%async_computation | async-start | bytes 1572864 | tf_op jit(solution)/shard_map/psum | solution.py:425
  218.3 3.2 %copy-start = (f32[3,256,256]{2,1,0:T(8,128)S(1)}, f32[3,256,256]{2,1,0:T(8,128)}, u32[]{:S(2)}) copy-start(f32[3,256,256]{2,1,0:T(8,128)} %all-reduce.2.cloned.1.call-done) | copy-start | bytes 2359300
Sparse Core Ops, SparseCore 0:
  120.9 97.3 all-reduce.1

commit v2 on v1

--- a/solution.py
+++ b/solution.py
@@ -21,7 +21,7 @@
     return jnp.dot(a, b, preferred_element_type=F32)
 
 
-def stage_list(num_layers):
+def stage_list(num_layers, nt):
     stages = []
     start = 0
     for layer in range(num_layers):
@@ -35,12 +35,16 @@
         stages.append(('by', layer, start + 2 * LAG))
         stages.append(('bx', layer, start + 2 * LAG + XLAG))
         start += 2 * LAG + XLAG
-    return stages, start
+    for kind, layer, first in list(stages):
+        if kind == 'bs':
+            stages += [('r%d' % phase, layer, first + nt - 1 + phase) for phase in range(7)]
+    return stages, max(first + (1 if kind[0] == 'r' else nt) for kind, _, first in stages)
 
 
 def kernel(sizes, vol, cot, taps, w, b, out, gw_out, gb_out,
-           vols, a1, a2, a3, gp, grad, d3, d2, d1, sb, yh, zh, zs, gb_acc,
+           vols, a1, a2, a3, gp, grad, d3, d2, d1, sb, yh, zh, zs,
            mfy, mfyh, mfz, mfzh, mby, mbyh, mbz, mbzh, sel,
+           gwx, rx, ry, rz, sum_send, sum_recv,
            in_sem, cot_sem, out_sem, ysend, yrecv, zsend, zrecv, xsend, xrecv):
     nx, ny, nz, num_layers, num_taps, by_len, bz_len = sizes
     half = (num_taps - 1) // 2
@@ -49,6 +53,9 @@
     edge_y = half * bz_len
     edge_z = half * by_len
     nt = planes // PLANES
+    part_x = w.shape[1] // nx
+    part_y = part_x // ny
+    part_z = part_y // nz
     my_x, my_y, my_z = lax.axis_index('gx'), lax.axis_index('gy'), lax.axis_index('gz')
     y_lo, y_hi = my_y > 0, my_y < ny - 1
     z_lo, z_hi = my_z > 0, my_z < nz - 1
@@ -74,10 +81,10 @@
 
     barrier = pltpu.get_barrier_semaphore()
     pl.semaphore_signal(barrier, inc=1, device_id=x_peer, device_id_type=MESH)
-    for has, device in ((y_lo, y_prev), (y_hi, y_next), (z_lo, z_prev), (z_hi, z_next)):
-        @pl.when(has)
-        def _():
-            pl.semaphore_signal(barrier, inc=1, device_id=device, device_id_type=MESH)
+    for offset in range(1, ny):
+        pl.semaphore_signal(barrier, inc=1, device_id={'gy': lax.rem(my_y + offset, ny)}, device_id_type=MESH)
+    for offset in range(1, nz):
+        pl.semaphore_signal(barrier, inc=1, device_id={'gz': lax.rem(my_z + offset, nz)}, device_id_type=MESH)
 
     def iota(shape, axis):
         return lax.broadcasted_iota(jnp.int32, shape, axis)
@@ -143,10 +150,9 @@
     zero_halo(yh, my_y == ny - 1, 1, edge_y)
     zero_halo(zh, my_z == 0, 0, edge_z)
     zero_halo(zh, my_z == nz - 1, 1, edge_z)
-    gw_out[...] = jnp.zeros(gw_out.shape, F32)
-    gb_acc[...] = jnp.zeros(gb_acc.shape, F32)
-
-    pl.semaphore_wait(barrier, 1 + y_lo.astype(jnp.int32) + y_hi.astype(jnp.int32) + z_lo.astype(jnp.int32) + z_hi.astype(jnp.int32))
+    gwx[...] = jnp.zeros(gwx.shape, F32)
+
+    pl.semaphore_wait(barrier, 1 + (ny - 1) + (nz - 1))
 
     def y_copies(src, stage, tau):
         at = pl.ds(tau * PLANES, PLANES)
@@ -294,16 +300,19 @@
                 acc = acc + scaled[:8] + scaled[8:]
             return acc
 
-        gb_acc[layer] = lax.fori_loop(0, rows // size, body, gb_acc[layer], unroll=2)
+        gwx[layer, 0, part_x:] = lax.fori_loop(0, rows // size, body, gwx[layer, 0, part_x:], unroll=2)
         for p in range(PLANES):
             j = tau * PLANES + p
             mixed = lax.dot_general(sb[p], w[layer], (((1,), (1,)), ((), ())), preferred_element_type=F32).astype(BF16)
             d3[j] = mixed
             zs[stage, j] = dot(sel[...], mixed).astype(BF16)
         start(z_copies(stage, tau))
-        for p in range(PLANES):
-            j = tau * PLANES + p
-            gw_out[layer] += lax.dot_general(a3[layer, j], sb[p], (((0,), (0,)), ((), ())), preferred_element_type=F32)
+        channels = w.shape[1]
+        product = lax.dot_general(
+            a3[layer, pl.ds(tau * PLANES, PLANES)].reshape(PLANES * rows, channels), sb[...].reshape(PLANES * rows, channels),
+            (((0,), (0,)), ((), ())), preferred_element_type=F32)
+        for side in range(nx):
+            gwx[layer, side, :part_x] += product[side * part_x:(side + 1) * part_x]
 
     def bz(layer, tau):
         stage = num_layers + layer
@@ -335,20 +344,101 @@
             for p in range(PLANES):
                 out_copy(tau * PLANES + p).start()
 
-    tasks = {'fx': fx, 'fy': fy, 'fz': fz, 'bs': bs, 'bz': bz, 'by': by, 'bx': bx}
-    stages, last = stage_list(num_layers)
+    def sum_copy(layer, phase, offset, src, dst, device):
+        return pltpu.make_async_remote_copy(
+            src_ref=src, dst_ref=dst, send_sem=sum_send.at[layer, phase, offset], recv_sem=sum_recv.at[layer, phase, offset],
+            device_id=device, device_id_type=MESH)
+
+    def phase_copies(layer, phase):
+        base_x = my_x * part_x
+        base_y = base_x + my_y * part_y
+        base_z = base_y + my_z * part_z
+        if phase == 0:
+            return [sum_copy(layer, 0, 0, gwx.at[layer, 1 - my_x], rx.at[layer], x_peer)]
+        if phase == 5:
+            at = pl.ds(pl.multiple_of(base_x, part_x), part_x)
+            return [sum_copy(layer, 5, 0, gw_out.at[layer, at], gw_out.at[layer, at], x_peer)]
+        copies = []
+        along_y = phase in (1, 4)
+        count, me, name = (ny, my_y, 'gy') if along_y else (nz, my_z, 'gz')
+        for offset in range(1, count):
+            other = lax.rem(me + offset, count)
+            if phase == 1:
+                src, dst = ry.at[layer, 1, other], ry.at[layer, 0, me]
+            elif phase == 2:
+                src, dst = rz.at[layer, 1, other], rz.at[layer, 0, me]
+            else:
+                at = pl.ds(pl.multiple_of(base_z, part_z), part_z) if phase == 3 else pl.ds(pl.multiple_of(base_y, part_y), part_y)
+                src, dst = gw_out.at[layer, at], gw_out.at[layer, at]
+            copies.append(sum_copy(layer, phase, offset - 1, src, dst, {name: other}))
+        return copies
+
+    def start_phase(layer, phase):
+        for copy in phase_copies(layer, phase):
+            copy.start()
+
+    def wait_phase(layer, phase):
+        for copy in phase_copies(layer, phase):
+            copy.wait()
+
+    def r0(layer, tau):
+        gwx[layer, 1, part_x:] = gwx[layer, 0, part_x:]
+        start_phase(layer, 0)
+
+    def spread(total, count, part, slots, layer, me):
+        bias = total[count * part:]
+        for k in range(count):
+            slots[layer, 1, k, :part] = total[k * part:(k + 1) * part]
+            slots[layer, 1, k, part:] = bias
+        slots[layer, 0, me] = slots[layer, 1, me]
+
+    def r1(layer, tau):
+        wait_phase(layer, 0)
+        spread(gwx[layer, my_x] + rx[layer], ny, part_y, ry, layer, my_y)
+        start_phase(layer, 1)
+
+    def gathered(slots, layer, count):
+        total = slots[layer, 0, 0]
+        for k in range(1, count):
+            total = total + slots[layer, 0, k]
+        return total
+
+    def r2(layer, tau):
+        wait_phase(layer, 1)
+        spread(gathered(ry, layer, ny), nz, part_z, rz, layer, my_z)
+        start_phase(layer, 2)
+
+    def r3(layer, tau):
+        wait_phase(layer, 2)
+        total = gathered(rz, layer, nz)
+        gw_out[layer, pl.ds(pl.multiple_of(my_x * part_x + my_y * part_y + my_z * part_z, part_z), part_z)] = total[:part_z]
+        gb_out[layer, :] = jnp.sum(total[part_z:], axis=0)
+        start_phase(layer, 3)
+
+    def r4(layer, tau):
+        wait_phase(layer, 3)
+        start_phase(layer, 4)
+
+    def r5(layer, tau):
+        wait_phase(layer, 4)
+        start_phase(layer, 5)
+
+    def r6(layer, tau):
+        wait_phase(layer, 5)
+
+    tasks = {'r0': r0, 'r1': r1, 'r2': r2, 'r3': r3, 'r4': r4, 'r5': r5, 'r6': r6, 'fx': fx, 'fy': fy, 'fz': fz, 'bs': bs, 'bz': bz, 'by': by, 'bx': bx}
+    stages, last = stage_list(num_layers, nt)
 
     def step(s, carry):
         for kind, layer, first in stages:
             tau = s - first
 
-            @pl.when((tau >= 0) & (tau < nt))
+            @pl.when((tau >= 0) & (tau < (1 if kind[0] == 'r' else nt)))
             def _():
                 tasks[kind](layer, tau)
         return carry
 
-    lax.fori_loop(0, last + nt, step, 0)
-    gb_out[...] = jnp.sum(gb_acc[...], axis=1)
+    lax.fori_loop(0, last, step, 0)
 
     def wait_out(j, carry):
         out_copy(j).wait()
@@ -371,6 +461,9 @@
         edge_y, edge_z = half * bz_len, half * by_len
         nt = planes // PLANES
         stages = 2 * num_layers
+        part_x = channels // nx
+        part_y = part_x // ny
+        part_z = part_y // nz
 
         def to_rows(block):
             return jnp.transpose(block, (1, 2, 3, 0)).reshape(planes, rows, channels)
@@ -403,7 +496,6 @@
                 pltpu.VMEM((stages, planes, 2 * edge_y, channels), BF16),
                 pltpu.VMEM((stages, planes, 2 * edge_z, channels), BF16),
                 pltpu.VMEM((stages, planes, 2 * edge_z, channels), BF16),
-                pltpu.VMEM((num_layers, 8, channels), F32),
                 pltpu.VMEM((num_layers, rows + 2 * edge_z, rows), BF16),
                 pltpu.VMEM((num_layers, rows + 2 * edge_z, 2 * edge_y), BF16),
                 pltpu.VMEM((num_layers, rows, rows), BF16),
@@ -413,6 +505,11 @@
                 pltpu.VMEM((num_layers, rows, rows), BF16),
                 pltpu.VMEM((num_layers, rows, 2 * edge_z), BF16),
                 pltpu.VMEM((2 * edge_z, rows), BF16),
+                pltpu.VMEM((num_layers, nx, part_x + 8, channels), F32),
+                pltpu.VMEM((num_layers, part_x + 8, channels), F32),
+                pltpu.VMEM((num_layers, 2, ny, part_y + 8, channels), F32),
+                pltpu.VMEM((num_layers, 2, nz, part_z + 8, channels), F32),
+                dma((num_layers, 6, max(ny, nz, 2) - 1)), dma((num_layers, 6, max(ny, nz, 2) - 1)),
                 dma((planes,)), dma((planes,)), dma((planes,)),
                 dma((stages, nt, 2)), dma((stages, nt, 2)), dma((stages, nt, 2)), dma((stages, nt, 2)),
                 dma((stages, half)), dma((stages, half)),
@@ -422,8 +519,6 @@
             name='stack',
         )(to_rows(volume), to_rows(cot_out), filter_taps.reshape(-1), w_mix, b_mix)
         grad_volume = jnp.transpose(grad_rows.reshape(planes, by_len, bz_len, channels), (3, 0, 1, 2))
-        grad_w_sum = lax.psum(grad_w, names)
-        grad_b_sum = lax.psum(grad_b, names)
-        return grad_volume, grad_w_sum, grad_b_sum
+        return grad_volume, grad_w, grad_b
 
     return jax.shard_map(local_step, mesh=mesh, in_specs=(vol_spec, vol_spec, P(), P(), P()), out_specs=(vol_spec, P('dp'), P('dp')), check_vma=False)

time: 230 us -> 144 us (0.63)
  waiting for transfers between devices: 50.9 us -> 0 us
  blocking collectives: 46.7 us -> 0 us
  Pallas kernels: 112 us -> 138 us
  between operations: 14.1 us -> 0.66 us
    psum x1 -> x0, waiting for transfers between devices: 50.8 us -> none  [local_step(): grad_w_sum = lax.psum(grad_w, names)]
    psum x1 -> x0, blocking collectives: 46.7 us -> none  [local_step(): grad_b_sum = lax.psum(grad_b, names)]
    pallas_call x1, Pallas kernels: 112 us -> 138 us  [local_step(): pl.pallas_call(functools.partial(kernel, (nx, ny, nz, num_layers, num_tap...]
    unnamed x4 -> x7, local copies, waits for them, and re-layouts: 4.05 us -> 4.65 us
  transfers between devices with their start and end apart: 1 -> 0, of which waited for: 1 -> 0; matrix products, arithmetic and copies ran while one was open for 0% -> 0% of each run, Pallas kernels for 0% -> 0%
where the time goes in v2:
time: 144 us
  Pallas kernels  138 us (96%)
  local copies, waits for them, and re-layouts  5.94 us (4%)
    pallas_call x1, Pallas kernels, local_step(): pl.pallas_call(functools.partial(kernel, (nx, ny, nz, num_layers, num_tap...  138 us
    unnamed x7, local copies, waits for them, and re-layouts  4.65 us

profile of v2, /device:TPU:97, one launch (start us, length us, event | category | flops | bytes accessed | tf_op | source)
XLA Modules:
  0.0 144.1 jit_solution(6035573791694709819)
XLA Ops:
  0.6 1.3 reshape.20.taps
  1.9 137.5 %stack.1 = (bf16[16,256,256]{2,1,0:T(8,128)(2,1)}, f32[3,256,256]{2,1,0:T(8,128)}, f32[3,256]{1,0:T(4,128)}) custom-call(bf16[16,256,256]{2,1,0:T(8,128)(2,1)} %bitcast.9, bf16[16,256,256]{2,1,0:T(8,128)(2,1)} %bitcast.10, f32[45]{0:T(128)} %reshape.20.taps, bf16[3,256,256]{2,1,0:T(8,128)(2,1)} %w.1, f32[3,256]{1,0:T(4,128)} %b.1), custom_call_target="tpu_custom_call" | custom-call | tf_op jit(solution)/shard_map/stack/pallas_call | solution.py:476
  139.5 0.0 copy-start
  139.5 0.0 copy-start.1
  139.5 3.2 %copy.11 = bf16[256,16,16,16]{0,3,2,1:T(8,128)(2,1)} copy(bf16[256,16,16,16]{0,3,2,1:T(8,128)(2,1)} %bitcast.11) | data formatting | bytes 4194304
  142.7 0.0 copy-done
  142.7 0.9 copy.12
  143.5 0.0 copy-done.1
  143.5 0.6 copy.13
Async XLA Ops:
  139.5 3.2 %copy-start = (f32[3,256,256]{2,1,0:T(8,128)S(1)}, f32[3,256,256]{2,1,0:T(8,128)}, u32[]{:S(2)}) copy-start(f32[3,256,256]{2,1,0:T(8,128)} %get-tuple-element.13) | copy-start | bytes 2359300
  139.5 4.1 %copy-start.1 = (f32[3,256]{1,0:T(4,128)S(1)}, f32[3,256]{1,0:T(4,128)}, u32[]{:S(2)}) copy-start(f32[3,256]{1,0:T(4,128)} %get-tuple-element.14) | copy-start | bytes 9220

commit v3 on v2

--- a/solution.py
+++ b/solution.py
@@ -9,11 +9,15 @@
 
 MESH = pl.DeviceIdType.MESH
 PLANES = 2
-LAG = 1
+LAG = 3
+SUM_LAG = 2
 XLAG = 1
 F32 = jnp.float32
 BF16 = jnp.bfloat16
 SQRT_HALF = 0.7071067811865476
+HALF_LOG2_E = 0.7213475204444817
+CHUNK = 16
+GROUP = 32
 INV_SQRT_2PI = 0.3989422804014327
 
 
@@ -37,13 +41,13 @@
         start += 2 * LAG + XLAG
     for kind, layer, first in list(stages):
         if kind == 'bs':
-            stages += [('r%d' % phase, layer, first + nt - 1 + phase) for phase in range(7)]
+            stages += [('r%d' % phase, layer, first + nt - 1 + phase * (SUM_LAG if layer else 1)) for phase in range(7)]
     return stages, max(first + (1 if kind[0] == 'r' else nt) for kind, _, first in stages)
 
 
 def kernel(sizes, vol, cot, taps, w, b, out, gw_out, gb_out,
            vols, a1, a2, a3, gp, grad, d3, d2, d1, sb, yh, zh, zs,
-           mfy, mfyh, mfz, mfzh, mby, mbyh, mbz, mbzh, sel,
+           mfx, mfy, mfz, mbx, mby, mbz, sel,
            gwx, rx, ry, rz, sum_send, sum_recv,
            in_sem, cot_sem, out_sem, ysend, yrecv, zsend, zrecv, xsend, xrecv):
     nx, ny, nz, num_layers, num_taps, by_len, bz_len = sizes
@@ -86,70 +90,65 @@
     for offset in range(1, nz):
         pl.semaphore_signal(barrier, inc=1, device_id={'gz': lax.rem(my_z + offset, nz)}, device_id_type=MESH)
 
+    half_y, half_rows = by_len // 2, rows // 2
+
     def iota(shape, axis):
         return lax.broadcasted_iota(jnp.int32, shape, axis)
 
-    def banded(layer, axis, back, diff, step, inside):
-        total = jnp.zeros(diff.shape, F32)
+    def banded(layer, axis, back, hop, inside):
+        total = jnp.zeros(hop.shape, F32)
         for t in range(num_taps):
-            tap = taps[(layer * 3 + axis) * num_taps + (num_taps - 1 - t if back else t)]
-            total = jnp.where(diff == step * (t - half), tap, total)
-        if inside is not None:
-            total = jnp.where(inside, total, 0.0)
-        return total.astype(BF16)
-
-    def build_chunk(chunk, carry):
-        size = 64
-        base = pl.multiple_of(chunk * size, size)
-        at = pl.ds(base, size)
-        halo_cols = 2 * edge_y
-        i_in, k_in = base + iota((size, rows), 0), iota((size, rows), 1)
-        i_halo, k_halo = base + iota((size, halo_cols), 0), iota((size, halo_cols), 1)
-        k_y = jnp.where(k_halo < edge_y, k_halo - edge_y, k_halo + rows - edge_y)
-        side = k_halo // edge_z
-        hop = (k_halo % edge_z) // by_len
-        zin = jnp.where(side == 0, hop - half, hop + bz_len)
-        same_y = k_halo % by_len == i_halo // bz_len
-        same_row = k_in // bz_len == i_in // bz_len
-        for layer in range(num_layers):
-            mfy[layer, at, :] = banded(layer, 1, False, k_in - i_in, bz_len, None)
-            mby[layer, at, :] = banded(layer, 1, True, k_in - i_in, bz_len, None)
-            mfyh[layer, at, :] = banded(layer, 1, False, k_y - i_halo, bz_len, None)
-            mbyh[layer, at, :] = banded(layer, 1, True, k_y - i_halo, bz_len, None)
-            mfz[layer, at, :] = banded(layer, 2, False, k_in - i_in, 1, same_row)
-            mbz[layer, at, :] = banded(layer, 2, True, k_in - i_in, 1, same_row)
-            mfzh[layer, at, :] = banded(layer, 2, False, zin - i_halo % bz_len, 1, same_y)
-            mbzh[layer, at, :] = banded(layer, 2, True, zin - i_halo % bz_len, 1, same_y)
+            tap = taps[layer, axis, num_taps - 1 - t if back else t]
+            if axis == 0:
+                tap = jnp.where(my_x == 1, tap, taps[layer, axis, t if back else num_taps - 1 - t])
+            total = jnp.where(hop == t, tap, total)
+        return jnp.where(inside, total, 0.0).astype(BF16)
+
+    def build(layer, carry):
+        i, k = iota((PLANES * GROUP, (PLANES + 2 * half) * GROUP), 0), iota((PLANES * GROUP, (PLANES + 2 * half) * GROUP), 1)
+        hop, inside = k // GROUP - i // GROUP, k % GROUP == i % GROUP
+        mfx[layer] = banded(layer, 0, False, hop, inside)
+        mbx[layer] = banded(layer, 0, True, hop, inside)
+        i, k = iota((half_rows, half_rows + 2 * edge_y), 0), iota((half_rows, half_rows + 2 * edge_y), 1)
+        hop, inside = k // bz_len - i // bz_len, k % bz_len == i % bz_len
+        mfy[layer, :half_rows] = banded(layer, 1, False, hop, inside)
+        mby[layer] = banded(layer, 1, True, hop, inside)
+        i, k = iota((edge_z, half_rows + 2 * edge_y), 0), iota((edge_z, half_rows + 2 * edge_y), 1)
+        z_edge = i // half_y % half + i // (half * half_y) * (bz_len - half)
+        mfy[layer, half_rows:] = banded(layer, 1, False, k // bz_len - i % half_y, k % bz_len == z_edge)
+        i, k = iota((half_rows, half_rows), 0), iota((half_rows, half_rows), 1)
+        hop, inside = k % bz_len - i % bz_len + half, k // bz_len == i // bz_len
+        mfz[layer, :, :half_rows] = banded(layer, 2, False, hop, inside)
+        mbz[layer, :, :half_rows] = banded(layer, 2, True, hop, inside)
+        i, k = iota((half_rows, edge_z), 0), iota((half_rows, edge_z), 1)
+        hop = k // half_y % half + k // (half * half_y) * (bz_len + half) - i % bz_len
+        inside = k % half_y == i // bz_len
+        mfz[layer, :, half_rows:] = banded(layer, 2, False, hop, inside)
+        mbz[layer, :, half_rows:] = banded(layer, 2, True, hop, inside)
         return carry
 
-    lax.fori_loop(0, rows // 64, build_chunk, 0)
-    q, k_in = iota((2 * edge_z, rows), 0), iota((2 * edge_z, rows), 1)
-    i_edge = (q % by_len) * bz_len + (q % edge_z) // by_len + (q // edge_z) * (bz_len - half)
-    sel[...] = jnp.where(k_in == i_edge, 1.0, 0.0).astype(BF16)
-    q, k_halo = iota((2 * edge_z, 2 * edge_y), 0), iota((2 * edge_z, 2 * edge_y), 1)
-    i_edge_h = (q % by_len) * bz_len + (q % edge_z) // by_len + (q // edge_z) * (bz_len - half)
-    k_y = jnp.where(k_halo < edge_y, k_halo - edge_y, k_halo + rows - edge_y)
-    for layer in range(num_layers):
-        mfy[layer, rows:, :] = banded(layer, 1, False, k_in - i_edge, bz_len, None)
-        mfyh[layer, rows:, :] = banded(layer, 1, False, k_y - i_edge_h, bz_len, None)
+    lax.fori_loop(0, num_layers, build, 0)
+    i, k = iota((edge_z, half_rows), 0), iota((edge_z, half_rows), 1)
+    z_edge = i // half_y % half + i // (half * half_y) * (bz_len - half)
+    sel[...] = jnp.where((k // bz_len == i % half_y) & (k % bz_len == z_edge), 1.0, 0.0).astype(BF16)
 
     for layer in range(num_layers):
         vols[layer, planes + half:] = jnp.zeros((half,) + vols.shape[2:], BF16)
         d1[layer, planes + half:] = jnp.zeros((half,) + d1.shape[2:], BF16)
 
-    def zero_halo(halo, where, side, edge):
+    def zero_halo(halo, where, side):
         @pl.when(where)
         def _():
             def clear(j, carry):
                 for stage in range(2 * num_layers):
-                    halo[stage, j, side * edge:(side + 1) * edge] = jnp.zeros((edge, halo.shape[3]), BF16)
+                    halo[stage, j, :, side] = jnp.zeros(halo.shape[2:3] + halo.shape[4:], BF16)
                 return carry
             lax.fori_loop(0, planes, clear, 0)
 
-    zero_halo(yh, my_y == 0, 0, edge_y)
-    zero_halo(yh, my_y == ny - 1, 1, edge_y)
-    zero_halo(zh, my_z == 0, 0, edge_z)
-    zero_halo(zh, my_z == nz - 1, 1, edge_z)
+    zero_halo(yh, my_y == 0, 0)
+    zero_halo(yh, my_y == ny - 1, 1)
+    zero_halo(zh, my_z == 0, 0)
+    zero_halo(zh, my_z == nz - 1, 1)
     gwx[...] = jnp.zeros(gwx.shape, F32)
 
     pl.semaphore_wait(barrier, 1 + (ny - 1) + (nz - 1))
@@ -157,20 +156,20 @@
     def y_copies(src, stage, tau):
         at = pl.ds(tau * PLANES, PLANES)
         up = pltpu.make_async_remote_copy(
-            src_ref=src.at[at, pl.ds(rows - edge_y, edge_y)], dst_ref=yh.at[stage, at, pl.ds(0, edge_y)],
+            src_ref=src.at[at, pl.ds(rows - edge_y, edge_y)], dst_ref=yh.at[stage, at, 0, 0],
             send_sem=ysend.at[stage, tau, 0], recv_sem=yrecv.at[stage, tau, 0], device_id=y_next, device_id_type=MESH)
         dn = pltpu.make_async_remote_copy(
-            src_ref=src.at[at, pl.ds(0, edge_y)], dst_ref=yh.at[stage, at, pl.ds(edge_y, edge_y)],
+            src_ref=src.at[at, pl.ds(0, edge_y)], dst_ref=yh.at[stage, at, 0, 1],
             send_sem=ysend.at[stage, tau, 1], recv_sem=yrecv.at[stage, tau, 1], device_id=y_prev, device_id_type=MESH)
         return up, dn, y_lo, y_hi
 
     def z_copies(stage, tau):
         at = pl.ds(tau * PLANES, PLANES)
         up = pltpu.make_async_remote_copy(
-            src_ref=zs.at[stage, at, pl.ds(edge_z, edge_z)], dst_ref=zh.at[stage, at, pl.ds(0, edge_z)],
+            src_ref=zs.at[stage, at, :, 1], dst_ref=zh.at[stage, at, :, 0],
             send_sem=zsend.at[stage, tau, 0], recv_sem=zrecv.at[stage, tau, 0], device_id=z_next, device_id_type=MESH)
         dn = pltpu.make_async_remote_copy(
-            src_ref=zs.at[stage, at, pl.ds(0, edge_z)], dst_ref=zh.at[stage, at, pl.ds(edge_z, edge_z)],
+            src_ref=zs.at[stage, at, :, 0], dst_ref=zh.at[stage, at, :, 1],
             send_sem=zsend.at[stage, tau, 1], recv_sem=zrecv.at[stage, tau, 1], device_id=z_prev, device_id_type=MESH)
         return up, dn, z_lo, z_hi
 
@@ -220,26 +219,25 @@
 
     lax.fori_loop(0, planes, wait_in, 0)
 
-    def x_tap(layer, back, u):
-        base = layer * 3 * num_taps
-        plain, flipped = taps[base + u], taps[base + num_taps - 1 - u]
-        return jnp.where(my_x == 1, flipped, plain) if back else jnp.where(my_x == 1, plain, flipped)
-
-    def x_pass(buf, layer, back, tau, emit):
-        weights = [x_tap(layer, back, u) for u in range(num_taps)]
-        size = 16
-
-        def body(chunk, carry):
-            at = pl.ds(pl.multiple_of(chunk * size, size), size)
-            loaded = [buf[layer, tau * PLANES + p, at, :].astype(F32) for p in range(PLANES + num_taps - 1)]
+    def x_pass(matrix, buf, layer, tau, emit):
+        for group in range(rows // GROUP):
+            at = pl.ds(group * GROUP, GROUP)
+            source = jnp.concatenate([buf[layer, tau * PLANES + p, at, :] for p in range(PLANES + 2 * half)], axis=0)
+            total = dot(matrix[layer], source)
             for p in range(PLANES):
-                total = weights[0] * loaded[p]
-                for u in range(1, num_taps):
-                    total = total + weights[u] * loaded[p + u]
-                emit(tau * PLANES + p, at, total)
-            return carry
-
-        lax.fori_loop(0, rows // size, body, 0, unroll=2)
+                emit(tau * PLANES + p, at, total[p * GROUP:(p + 1) * GROUP])
+
+    def y_source(buf, stage, j, part):
+        if part == 0:
+            return jnp.concatenate([yh[stage, j, 0, 0], buf[j, :half_rows + edge_y]], axis=0)
+        return jnp.concatenate([buf[j, half_rows - edge_y:], yh[stage, j, 0, 1]], axis=0)
+
+    def z_source(buf, stage, j, part):
+        halo = zh[stage, j, part]
+        return jnp.concatenate([buf[j, part * half_rows:(part + 1) * half_rows], halo.reshape(edge_z, halo.shape[2])], axis=0)
+
+    def put_z_edge(stage, j, part, value):
+        zs[stage, j, part] = value.reshape(zs.shape[3:])
 
     def fx(layer, tau):
         wait_x(vols, layer, layer, tau)
@@ -247,40 +245,36 @@
         def emit(j, at, total):
             a1[j, at, :] = total.astype(BF16)
 
-        x_pass(vols, layer, False, tau, emit)
+        x_pass(mfx, vols, layer, tau, emit)
         start(y_copies(a1, layer, tau))
 
     def fy(layer, tau):
         wait(y_copies(a1, layer, tau))
         for p in range(PLANES):
             j = tau * PLANES + p
-            total = dot(mfy[layer], a1[j]) + dot(mfyh[layer], yh[layer, j])
-            a2[j] = total[:rows].astype(BF16)
-            zs[layer, j] = total[rows:].astype(BF16)
+            for part in range(2):
+                total = dot(mfy[layer], y_source(a1, layer, j, part)).astype(BF16)
+                a2[j, part * half_rows:(part + 1) * half_rows] = total[:half_rows]
+                put_z_edge(layer, j, part, total[half_rows:])
         start(z_copies(layer, tau))
 
     def fz(layer, tau):
         wait(z_copies(layer, tau))
+        bias = b[layer, :][None, :]
         for p in range(PLANES):
             j = tau * PLANES + p
-            total = dot(mfz[layer], a2[j]) + dot(mfzh[layer], zh[layer, j])
-            filtered = total.astype(BF16)
-            a3[layer, j] = filtered
-            gp[layer, j] = dot(filtered, w[layer]) + b[layer, :][None, :]
-        size = 16
-
-        def body(chunk, carry):
-            at = pl.ds(pl.multiple_of(chunk * size, size), size)
-            for p in range(PLANES):
-                j = tau * PLANES + p
-                z = gp[layer, j, at, :]
-                cdf = 0.5 * (1.0 + lax.erf(z * SQRT_HALF))
-                gp[layer, j, at, :] = cdf + z * (jnp.exp(-0.5 * (z * z)) * INV_SQRT_2PI)
-                if layer + 1 < num_layers:
-                    vols[layer + 1, j + half, at, :] = (vols[layer, j + half, at, :].astype(F32) + z * cdf).astype(BF16)
-            return carry
-
-        lax.fori_loop(0, rows // size, body, 0, unroll=2)
+            for part in range(2):
+                at = slice(part * half_rows, (part + 1) * half_rows)
+                filtered = dot(mfz[layer], z_source(a2, layer, j, part)).astype(BF16)
+                a3[layer, j, at] = filtered
+                pre = dot(filtered, w[layer])
+                for first in range(0, half_rows, CHUNK):
+                    at = slice(part * half_rows + first, part * half_rows + first + CHUNK)
+                    z = pre[first:first + CHUNK] + bias
+                    cdf = 0.5 * lax.erf(z * SQRT_HALF) + 0.5
+                    gp[layer, j, at] = cdf + z * (jnp.exp2((z * z) * -HALF_LOG2_E) * INV_SQRT_2PI)
+                    if layer + 1 < num_layers:
+                        vols[layer + 1, j + half, at] = (vols[layer, j + half, at].astype(F32) + z * cdf).astype(BF16)
         if layer + 1 < num_layers:
             start_x(vols, layer + 1, layer + 1, tau)
 
@@ -289,23 +283,23 @@
         if layer == num_layers - 1:
             for p in range(PLANES):
                 cot_copy(tau * PLANES + p).wait()
-        size = 16
-
-        def body(chunk, acc):
-            at = pl.ds(pl.multiple_of(chunk * size, size), size)
-            for p in range(PLANES):
-                j = tau * PLANES + p
-                scaled = gp[layer, j, at, :] * grad[j, at, :].astype(F32)
-                sb[p, at, :] = scaled.astype(BF16)
-                acc = acc + scaled[:8] + scaled[8:]
-            return acc
-
-        gwx[layer, 0, part_x:] = lax.fori_loop(0, rows // size, body, gwx[layer, 0, part_x:], unroll=2)
+        total_b = gwx[layer, 0, part_x:]
         for p in range(PLANES):
             j = tau * PLANES + p
-            mixed = lax.dot_general(sb[p], w[layer], (((1,), (1,)), ((), ())), preferred_element_type=F32).astype(BF16)
-            d3[j] = mixed
-            zs[stage, j] = dot(sel[...], mixed).astype(BF16)
+            for part in range(2):
+                chunks = []
+                for first in range(part * half_rows, (part + 1) * half_rows, CHUNK):
+                    at = slice(first, first + CHUNK)
+                    scaled = gp[layer, j, at] * grad[j, at].astype(F32)
+                    total_b = total_b + jnp.sum(scaled.reshape(CHUNK // 8, 8, scaled.shape[1]), axis=0)
+                    chunks.append(scaled.astype(BF16))
+                    sb[p, at] = chunks[-1]
+                at = slice(part * half_rows, (part + 1) * half_rows)
+                rounded = jnp.concatenate(chunks, axis=0)
+                mixed = lax.dot_general(rounded, w[layer], (((1,), (1,)), ((), ())), preferred_element_type=F32).astype(BF16)
+                d3[j, at] = mixed
+                put_z_edge(stage, j, part, dot(sel[...], mixed).astype(BF16))
+        gwx[layer, 0, part_x:] = total_b
         start(z_copies(stage, tau))
         channels = w.shape[1]
         product = lax.dot_general(
@@ -319,7 +313,8 @@
         wait(z_copies(stage, tau))
         for p in range(PLANES):
             j = tau * PLANES + p
-            d2[j] = (dot(mbz[layer], d3[j]) + dot(mbzh[layer], zh[stage, j])).astype(BF16)
+            for part in range(2):
+                d2[j, part * half_rows:(part + 1) * half_rows] = dot(mbz[layer], z_source(d3, stage, j, part)).astype(BF16)
         start(y_copies(d2, stage, tau))
 
     def by(layer, tau):
@@ -327,7 +322,8 @@
         wait(y_copies(d2, stage, tau))
         for p in range(PLANES):
             j = tau * PLANES + p
-            d1[layer, j + half] = (dot(mby[layer], d2[j]) + dot(mbyh[layer], yh[stage, j])).astype(BF16)
+            for part in range(2):
+                d1[layer, j + half, part * half_rows:(part + 1) * half_rows] = dot(mby[layer], y_source(d2, stage, j, part)).astype(BF16)
         start_x(d1, stage, layer, tau)
 
     def out_copy(j):
@@ -339,7 +335,7 @@
         def emit(j, at, total):
             grad[j, at, :] = (grad[j, at, :].astype(F32) + total).astype(BF16)
 
-        x_pass(d1, layer, True, tau, emit)
+        x_pass(mbx, d1, layer, tau, emit)
         if layer == 0:
             for p in range(PLANES):
                 out_copy(tau * PLANES + p).start()
@@ -493,18 +489,16 @@
                 pltpu.VMEM(block, BF16),
                 pltpu.VMEM((num_layers, planes + 2 * half, rows, channels), BF16),
                 pltpu.VMEM((PLANES, rows, channels), BF16),
-                pltpu.VMEM((stages, planes, 2 * edge_y, channels), BF16),
-                pltpu.VMEM((stages, planes, 2 * edge_z, channels), BF16),
-                pltpu.VMEM((stages, planes, 2 * edge_z, channels), BF16),
-                pltpu.VMEM((num_layers, rows + 2 * edge_z, rows), BF16),
-                pltpu.VMEM((num_layers, rows + 2 * edge_z, 2 * edge_y), BF16),
-                pltpu.VMEM((num_layers, rows, rows), BF16),
-                pltpu.VMEM((num_layers, rows, 2 * edge_z), BF16),
-                pltpu.VMEM((num_layers, rows, rows), BF16),
-                pltpu.VMEM((num_layers, rows, 2 * edge_y), BF16),
-                pltpu.VMEM((num_layers, rows, rows), BF16),
-                pltpu.VMEM((num_layers, rows, 2 * edge_z), BF16),
-                pltpu.VMEM((2 * edge_z, rows), BF16),
+                pltpu.VMEM((stages, planes, 1, 2, edge_y, channels), BF16),
+                pltpu.VMEM((stages, planes, 2, 2, edge_z // 2, channels), BF16),
+                pltpu.VMEM((stages, planes, 2, 2, edge_z // 2, channels), BF16),
+                pltpu.VMEM((num_layers, PLANES * GROUP, (PLANES + 2 * half) * GROUP), BF16),
+                pltpu.VMEM((num_layers, rows // 2 + edge_z, rows // 2 + 2 * edge_y), BF16),
+                pltpu.VMEM((num_layers, rows // 2, rows // 2 + edge_z), BF16),
+                pltpu.VMEM((num_layers, PLANES * GROUP, (PLANES + 2 * half) * GROUP), BF16),
+                pltpu.VMEM((num_layers, rows // 2, rows // 2 + 2 * edge_y), BF16),
+                pltpu.VMEM((num_layers, rows // 2, rows // 2 + edge_z), BF16),
+                pltpu.VMEM((edge_z, rows // 2), BF16),
                 pltpu.VMEM((num_layers, nx, part_x + 8, channels), F32),
                 pltpu.VMEM((num_layers, part_x + 8, channels), F32),
                 pltpu.VMEM((num_layers, 2, ny, part_y + 8, channels), F32),
@@ -517,7 +511,7 @@
             compiler_params=pltpu.CompilerParams(
                 collective_id=0, has_side_effects=True, vmem_limit_bytes=64000 * 1024),
             name='stack',
-        )(to_rows(volume), to_rows(cot_out), filter_taps.reshape(-1), w_mix, b_mix)
+        )(to_rows(volume), to_rows(cot_out), filter_taps, w_mix, b_mix)
         grad_volume = jnp.transpose(grad_rows.reshape(planes, by_len, bz_len, channels), (3, 0, 1, 2))
         return grad_volume, grad_w, grad_b
 

time: 144 us -> 124 us (0.86)
  Pallas kernels: 138 us -> 118 us
    pallas_call x1, Pallas kernels: 138 us -> 118 us  [local_step(): pl.pallas_call(functools.partial(kernel, (nx, ny, nz, num_layers, num_tap...]
where the time goes in v3:
time: 124 us; the launch traced here: 123 us
  Pallas kernels  118 us (95%)
  local copies, waits for them, and re-layouts  4.65 us (4%)
    pallas_call x1, Pallas kernels, local_step(): pl.pallas_call(functools.partial(kernel, (nx, ny, nz, num_layers, num_tap...  118 us
    unnamed x7, local copies, waits for them, and re-layouts  4.65 us

profile of v3, /device:TPU:97, one launch (start us, length us, event | category | flops | bytes accessed | tf_op | source)
XLA Modules:
  0.0 123.5 jit_solution(16321272902595341629)
XLA Ops:
  0.6 118.1 %stack.1 = (bf16[16,256,256]{2,1,0:T(8,128)(2,1)}, f32[3,256,256]{2,1,0:T(8,128)}, f32[3,256]{1,0:T(4,128)}) custom-call(bf16[16,256,256]{2,1,0:T(8,128)(2,1)} %bitcast.9, bf16[16,256,256]{2,1,0:T(8,128)(2,1)} %bitcast.10, f32[3,3,5]{2,1,0:T(4,128)} %taps.1, bf16[3,256,256]{2,1,0:T(8,128)(2,1)} %w.1, f32[3,256]{1,0:T(4,128)} %b.1), custom_call_target="tpu_custom_call" | custom-call | tf_op jit(solution)/shard_map/stack/pallas_call | solution.py:472
  118.8 0.0 copy-start
  118.8 0.0 copy-start.1
  118.8 3.2 %copy.11 = bf16[256,16,16,16]{0,3,2,1:T(8,128)(2,1)} copy(bf16[256,16,16,16]{0,3,2,1:T(8,128)(2,1)} %bitcast.11) | data formatting | bytes 4194304
  122.0 0.0 copy-done
  122.0 0.9 copy.12
  122.9 0.0 copy-done.1
  122.9 0.6 copy.13
Async XLA Ops:
  118.8 3.2 %copy-start = (f32[3,256,256]{2,1,0:T(8,128)S(1)}, f32[3,256,256]{2,1,0:T(8,128)}, u32[]{:S(2)}) copy-start(f32[3,256,256]{2,1,0:T(8,128)} %get-tuple-element.13) | copy-start | bytes 2359300
  118.8 4.1 %copy-start.1 = (f32[3,256]{1,0:T(4,128)S(1)}, f32[3,256]{1,0:T(4,128)}, u32[]{:S(2)}) copy-start(f32[3,256]{1,0:T(4,128)} %get-tuple-element.14) | copy-start | bytes 9220

commit v4 on v3

--- a/solution.py
+++ b/solution.py
@@ -10,7 +10,8 @@
 MESH = pl.DeviceIdType.MESH
 PLANES = 2
 LAG = 3
-SUM_LAG = 2
+SUM_STEPS = (0, 2, 6, 10, 12)
+LAST_SUM_STEPS = (0, 1, 6, 8, 9)
 XLAG = 1
 F32 = jnp.float32
 BF16 = jnp.bfloat16
@@ -41,14 +42,14 @@
         start += 2 * LAG + XLAG
     for kind, layer, first in list(stages):
         if kind == 'bs':
-            stages += [('r%d' % phase, layer, first + nt - 1 + phase * (SUM_LAG if layer else 1)) for phase in range(7)]
+            stages += [('r%d' % phase, layer, first + nt - 1 + (SUM_STEPS if layer else LAST_SUM_STEPS)[phase]) for phase in range(5)]
     return stages, max(first + (1 if kind[0] == 'r' else nt) for kind, _, first in stages)
 
 
 def kernel(sizes, vol, cot, taps, w, b, out, gw_out, gb_out,
            vols, a1, a2, a3, gp, grad, d3, d2, d1, sb, yh, zh, zs,
            mfx, mfy, mfz, mbx, mby, mbz, sel,
-           gwx, rx, ry, rz, sum_send, sum_recv,
+           gwx, rx, rq, sum_send, sum_recv,
            in_sem, cot_sem, out_sem, ysend, yrecv, zsend, zrecv, xsend, xrecv):
     nx, ny, nz, num_layers, num_taps, by_len, bz_len = sizes
     half = (num_taps - 1) // 2
@@ -58,8 +59,8 @@
     edge_z = half * by_len
     nt = planes // PLANES
     part_x = w.shape[1] // nx
-    part_y = part_x // ny
-    part_z = part_y // nz
+    group = ny * nz
+    part_q = part_x // group
     my_x, my_y, my_z = lax.axis_index('gx'), lax.axis_index('gy'), lax.axis_index('gz')
     y_lo, y_hi = my_y > 0, my_y < ny - 1
     z_lo, z_hi = my_z > 0, my_z < nz - 1
@@ -70,6 +71,20 @@
     def x_of(j):
         return my_x * j + (1 - my_x) * (planes - 1 - j)
 
+    my_q = my_z * ny + my_y
+
+    def chip(q):
+        return {'gy': lax.rem(q, ny), 'gz': q // ny}
+
+    barrier = pltpu.get_barrier_semaphore()
+    pl.semaphore_signal(barrier, inc=1, device_id=x_peer, device_id_type=MESH)
+
+    def signal_chip(offset, carry):
+        pl.semaphore_signal(barrier, inc=1, device_id=chip(lax.rem(my_q + offset, group)), device_id_type=MESH)
+        return carry
+
+    lax.fori_loop(1, group, signal_chip, 0)
+
     def in_copy(j):
         return pltpu.make_async_copy(vol.at[x_of(j)], vols.at[0, j + half], in_sem.at[j])
 
@@ -82,13 +97,6 @@
         return carry
 
     lax.fori_loop(0, planes, start_in, 0)
-
-    barrier = pltpu.get_barrier_semaphore()
-    pl.semaphore_signal(barrier, inc=1, device_id=x_peer, device_id_type=MESH)
-    for offset in range(1, ny):
-        pl.semaphore_signal(barrier, inc=1, device_id={'gy': lax.rem(my_y + offset, ny)}, device_id_type=MESH)
-    for offset in range(1, nz):
-        pl.semaphore_signal(barrier, inc=1, device_id={'gz': lax.rem(my_z + offset, nz)}, device_id_type=MESH)
 
     half_y, half_rows = by_len // 2, rows // 2
 
@@ -151,7 +159,7 @@
     zero_halo(zh, my_z == nz - 1, 1)
     gwx[...] = jnp.zeros(gwx.shape, F32)
 
-    pl.semaphore_wait(barrier, 1 + (ny - 1) + (nz - 1))
+    pl.semaphore_wait(barrier, group)
 
     def y_copies(src, stage, tau):
         at = pl.ds(tau * PLANES, PLANES)
@@ -345,84 +353,58 @@
             src_ref=src, dst_ref=dst, send_sem=sum_send.at[layer, phase, offset], recv_sem=sum_recv.at[layer, phase, offset],
             device_id=device, device_id_type=MESH)
 
-    def phase_copies(layer, phase):
-        base_x = my_x * part_x
-        base_y = base_x + my_y * part_y
-        base_z = base_y + my_z * part_z
+    def core_copy(layer, phase):
         if phase == 0:
-            return [sum_copy(layer, 0, 0, gwx.at[layer, 1 - my_x], rx.at[layer], x_peer)]
-        if phase == 5:
-            at = pl.ds(pl.multiple_of(base_x, part_x), part_x)
-            return [sum_copy(layer, 5, 0, gw_out.at[layer, at], gw_out.at[layer, at], x_peer)]
-        copies = []
-        along_y = phase in (1, 4)
-        count, me, name = (ny, my_y, 'gy') if along_y else (nz, my_z, 'gz')
-        for offset in range(1, count):
-            other = lax.rem(me + offset, count)
-            if phase == 1:
-                src, dst = ry.at[layer, 1, other], ry.at[layer, 0, me]
-            elif phase == 2:
-                src, dst = rz.at[layer, 1, other], rz.at[layer, 0, me]
-            else:
-                at = pl.ds(pl.multiple_of(base_z, part_z), part_z) if phase == 3 else pl.ds(pl.multiple_of(base_y, part_y), part_y)
-                src, dst = gw_out.at[layer, at], gw_out.at[layer, at]
-            copies.append(sum_copy(layer, phase, offset - 1, src, dst, {name: other}))
-        return copies
-
-    def start_phase(layer, phase):
-        for copy in phase_copies(layer, phase):
-            copy.start()
-
-    def wait_phase(layer, phase):
-        for copy in phase_copies(layer, phase):
-            copy.wait()
+            return sum_copy(layer, 0, 0, gwx.at[layer, 1 - my_x], rx.at[layer], x_peer)
+        at = pl.ds(pl.multiple_of(my_x * part_x, part_x), part_x)
+        return sum_copy(layer, 3, 0, gw_out.at[layer, at], gw_out.at[layer, at], x_peer)
+
+    def own_rows():
+        return pl.ds(pl.multiple_of(my_x * part_x + my_q * part_q, part_q), part_q)
+
+    def chip_copy(layer, phase, offset):
+        other = lax.rem(my_q + offset, group)
+        if phase == 1:
+            return sum_copy(layer, 1, offset, rq.at[layer, 1, other], rq.at[layer, 0, my_q], chip(other))
+        return sum_copy(layer, 2, offset, gw_out.at[layer, own_rows()], gw_out.at[layer, own_rows()], chip(other))
+
+    def each_chip(layer, phase, act):
+        def body(offset, carry):
+            act(chip_copy(layer, phase, offset))
+            return carry
+        lax.fori_loop(1, group, body, 0)
 
     def r0(layer, tau):
         gwx[layer, 1, part_x:] = gwx[layer, 0, part_x:]
-        start_phase(layer, 0)
-
-    def spread(total, count, part, slots, layer, me):
-        bias = total[count * part:]
-        for k in range(count):
-            slots[layer, 1, k, :part] = total[k * part:(k + 1) * part]
-            slots[layer, 1, k, part:] = bias
-        slots[layer, 0, me] = slots[layer, 1, me]
+        core_copy(layer, 0).start()
 
     def r1(layer, tau):
-        wait_phase(layer, 0)
-        spread(gwx[layer, my_x] + rx[layer], ny, part_y, ry, layer, my_y)
-        start_phase(layer, 1)
-
-    def gathered(slots, layer, count):
-        total = slots[layer, 0, 0]
-        for k in range(1, count):
-            total = total + slots[layer, 0, k]
-        return total
+        core_copy(layer, 0).wait()
+        bias = gwx[layer, my_x, part_x:] + rx[layer, part_x:]
+        for q in range(group):
+            at = slice(q * part_q, (q + 1) * part_q)
+            rq[layer, 1, q, :part_q] = gwx[layer, my_x, at] + rx[layer, at]
+            rq[layer, 1, q, part_q:] = bias
+        rq[layer, 0, my_q] = rq[layer, 1, my_q]
+        each_chip(layer, 1, lambda copy: copy.start())
 
     def r2(layer, tau):
-        wait_phase(layer, 1)
-        spread(gathered(ry, layer, ny), nz, part_z, rz, layer, my_z)
-        start_phase(layer, 2)
+        each_chip(layer, 1, lambda copy: copy.wait())
+        total = rq[layer, 0, 0]
+        for q in range(1, group):
+            total = total + rq[layer, 0, q]
+        gw_out[layer, own_rows()] = total[:part_q]
+        gb_out[layer, :] = jnp.sum(total[part_q:], axis=0)
+        each_chip(layer, 2, lambda copy: copy.start())
 
     def r3(layer, tau):
-        wait_phase(layer, 2)
-        total = gathered(rz, layer, nz)
-        gw_out[layer, pl.ds(pl.multiple_of(my_x * part_x + my_y * part_y + my_z * part_z, part_z), part_z)] = total[:part_z]
-        gb_out[layer, :] = jnp.sum(total[part_z:], axis=0)
-        start_phase(layer, 3)
+        each_chip(layer, 2, lambda copy: copy.wait())
+        core_copy(layer, 3).start()
 
     def r4(layer, tau):
-        wait_phase(layer, 3)
-        start_phase(layer, 4)
-
-    def r5(layer, tau):
-        wait_phase(layer, 4)
-        start_phase(layer, 5)
-
-    def r6(layer, tau):
-        wait_phase(layer, 5)
-
-    tasks = {'r0': r0, 'r1': r1, 'r2': r2, 'r3': r3, 'r4': r4, 'r5': r5, 'r6': r6, 'fx': fx, 'fy': fy, 'fz': fz, 'bs': bs, 'bz': bz, 'by': by, 'bx': bx}
+        core_copy(layer, 3).wait()
+
+    tasks = {'r0': r0, 'r1': r1, 'r2': r2, 'r3': r3, 'r4': r4, 'fx': fx, 'fy': fy, 'fz': fz, 'bs': bs, 'bz': bz, 'by': by, 'bx': bx}
     stages, last = stage_list(num_layers, nt)
 
     def step(s, carry):
@@ -458,8 +440,7 @@
         nt = planes // PLANES
         stages = 2 * num_layers
         part_x = channels // nx
-        part_y = part_x // ny
-        part_z = part_y // nz
+        part_q = part_x // (ny * nz)
 
         def to_rows(block):
             return jnp.transpose(block, (1, 2, 3, 0)).reshape(planes, rows, channels)
@@ -501,9 +482,8 @@
                 pltpu.VMEM((edge_z, rows // 2), BF16),
                 pltpu.VMEM((num_layers, nx, part_x + 8, channels), F32),
                 pltpu.VMEM((num_layers, part_x + 8, channels), F32),
-                pltpu.VMEM((num_layers, 2, ny, part_y + 8, channels), F32),
-                pltpu.VMEM((num_layers, 2, nz, part_z + 8, channels), F32),
-                dma((num_layers, 6, max(ny, nz, 2) - 1)), dma((num_layers, 6, max(ny, nz, 2) - 1)),
+                pltpu.VMEM((num_layers, 2, ny * nz, part_q + 8, channels), F32),
+                dma((num_layers, 4, ny * nz)), dma((num_layers, 4, ny * nz)),
                 dma((planes,)), dma((planes,)), dma((planes,)),
                 dma((stages, nt, 2)), dma((stages, nt, 2)), dma((stages, nt, 2)), dma((stages, nt, 2)),
                 dma((stages, half)), dma((stages, half)),

time: 124 us -> 121 us (0.976)
  Pallas kernels: 118 us -> 115 us
    pallas_call x1, Pallas kernels: 118 us -> 115 us  [local_step(): pl.pallas_call(functools.partial(kernel, (nx, ny, nz, num_layers, num_tap...]
where the time goes in v4:
time: 121 us
  Pallas kernels  115 us (95%)
  local copies, waits for them, and re-layouts  4.65 us (4%)
    pallas_call x1, Pallas kernels, local_step(): pl.pallas_call(functools.partial(kernel, (nx, ny, nz, num_layers, num_tap...  115 us
    unnamed x7, local copies, waits for them, and re-layouts  4.65 us

profile of v4, /device:TPU:97, one launch (start us, length us, event | category | flops | bytes accessed | tf_op | source)
XLA Modules:
  0.0 120.7 jit_solution(5389578727524010279)
XLA Ops:
  0.6 115.4 %stack.1 = (bf16[16,256,256]{2,1,0:T(8,128)(2,1)}, f32[3,256,256]{2,1,0:T(8,128)}, f32[3,256]{1,0:T(4,128)}) custom-call(bf16[16,256,256]{2,1,0:T(8,128)(2,1)} %bitcast.9, bf16[16,256,256]{2,1,0:T(8,128)(2,1)} %bitcast.10, f32[3,3,5]{2,1,0:T(4,128)} %taps.1, bf16[3,256,256]{2,1,0:T(8,128)(2,1)} %w.1, f32[3,256]{1,0:T(4,128)} %b.1), custom_call_target="tpu_custom_call" | custom-call | tf_op jit(solution)/shard_map/stack/pallas_call | solution.py:453
  116.0 0.0 copy-start
  116.0 0.0 copy-start.1
  116.0 3.2 %copy.11 = bf16[256,16,16,16]{0,3,2,1:T(8,128)(2,1)} copy(bf16[256,16,16,16]{0,3,2,1:T(8,128)(2,1)} %bitcast.11) | data formatting | bytes 4194304
  119.2 0.0 copy-done
  119.2 0.9 copy.12
  120.1 0.0 copy-done.1
  120.1 0.6 copy.13
Async XLA Ops:
  116.0 3.2 %copy-start = (f32[3,256,256]{2,1,0:T(8,128)S(1)}, f32[3,256,256]{2,1,0:T(8,128)}, u32[]{:S(2)}) copy-start(f32[3,256,256]{2,1,0:T(8,128)} %get-tuple-element.13) | copy-start | bytes 2359300
  116.0 4.1 %copy-start.1 = (f32[3,256]{1,0:T(4,128)S(1)}, f32[3,256]{1,0:T(4,128)}, u32[]{:S(2)}) copy-start(f32[3,256]{1,0:T(4,128)} %get-tuple-element.14) | copy-start | bytes 9220

commit v5 on v4

--- a/solution.py
+++ b/solution.py
@@ -8,10 +8,10 @@
 from jax.sharding import PartitionSpec as P
 
 MESH = pl.DeviceIdType.MESH
-PLANES = 2
-LAG = 3
-SUM_STEPS = (0, 2, 6, 10, 12)
-LAST_SUM_STEPS = (0, 1, 6, 8, 9)
+PLANES = 4
+LAG = 2
+SUM_STEPS = (0, 1, 3, 5, 6)
+LAST_SUM_STEPS = (0, 1, 3, 5, 6)
 XLAG = 1
 F32 = jnp.float32
 BF16 = jnp.bfloat16

time: 121 us -> 110 us (0.909)
  Pallas kernels: 115 us -> 105 us
    pallas_call x1, Pallas kernels: 115 us -> 105 us  [local_step(): pl.pallas_call(functools.partial(kernel, (nx, ny, nz, num_layers, num_tap...]
where the time goes in v5:
time: 110 us
  Pallas kernels  105 us (95%)
  local copies, waits for them, and re-layouts  4.65 us (4%)
    pallas_call x1, Pallas kernels, local_step(): pl.pallas_call(functools.partial(kernel, (nx, ny, nz, num_layers, num_tap...  105 us
    unnamed x7, local copies, waits for them, and re-layouts  4.65 us

profile of v5, /device:TPU:97, one launch (start us, length us, event | category | flops | bytes accessed | tf_op | source)
XLA Modules:
  0.0 110.2 jit_solution(11752773216051340466)
XLA Ops:
  0.6 104.9 %stack.1 = (bf16[16,256,256]{2,1,0:T(8,128)(2,1)}, f32[3,256,256]{2,1,0:T(8,128)}, f32[3,256]{1,0:T(4,128)}) custom-call(bf16[16,256,256]{2,1,0:T(8,128)(2,1)} %bitcast.9, bf16[16,256,256]{2,1,0:T(8,128)(2,1)} %bitcast.10, f32[3,3,5]{2,1,0:T(4,128)} %taps.1, bf16[3,256,256]{2,1,0:T(8,128)(2,1)} %w.1, f32[3,256]{1,0:T(4,128)} %b.1), custom_call_target="tpu_custom_call" | custom-call | tf_op jit(solution)/shard_map/stack/pallas_call | solution.py:453
  105.5 0.0 copy-start
  105.5 0.0 copy-start.1
  105.5 3.2 %copy.11 = bf16[256,16,16,16]{0,3,2,1:T(8,128)(2,1)} copy(bf16[256,16,16,16]{0,3,2,1:T(8,128)(2,1)} %bitcast.11) | data formatting | bytes 4194304
  108.7 0.0 copy-done
  108.7 0.9 copy.12
  109.6 0.0 copy-done.1
  109.6 0.6 copy.13
Async XLA Ops:
  105.5 3.2 %copy-start = (f32[3,256,256]{2,1,0:T(8,128)S(1)}, f32[3,256,256]{2,1,0:T(8,128)}, u32[]{:S(2)}) copy-start(f32[3,256,256]{2,1,0:T(8,128)} %get-tuple-element.13) | copy-start | bytes 2359300
  105.5 4.1 %copy-start.1 = (f32[3,256]{1,0:T(4,128)S(1)}, f32[3,256]{1,0:T(4,128)}, u32[]{:S(2)}) copy-start(f32[3,256]{1,0:T(4,128)} %get-tuple-element.14) | copy-start | bytes 9220

commit v6 on v5

v6 whole, which is shorter than its diff:
```python
import functools

import jax
import jax.numpy as jnp
from jax import lax
from jax.experimental import pallas as pl
from jax.experimental.pallas import tpu as pltpu
from jax.sharding import PartitionSpec as P

MESH = pl.DeviceIdType.MESH
PLANES = 4
LAG = 2
SUM_STEPS = ((0, 1, 2, 3, 4), (0, 2, 5, 7, 8), (0, 2, 5, 7, 9))
XLAG = 1
F32 = jnp.float32
BF16 = jnp.bfloat16
SQRT_HALF = 0.7071067811865476
HALF_LOG2_E = 0.7213475204444817
CHUNK = 16
INV_SQRT_2PI = 0.3989422804014327


def dot(a, b):
    return jnp.dot(a, b, preferred_element_type=F32)


def stage_list(num_layers, nt):
    stages = []
    start = 0
    for layer in range(num_layers):
        stages.append(('fx', layer, start))
        stages.append(('fz', layer, start + LAG))
        start += LAG + (XLAG if layer + 1 < num_layers else 0)
    for layer in reversed(range(num_layers)):
        stages.append(('bs', layer, start))
        stages.append(('by', layer, start + LAG))
        stages.append(('bx', layer, start + LAG + XLAG))
        start += LAG + XLAG
    stages[1:1] = [('m', layer, layer) for layer in range(num_layers)]
    for kind, layer, first in list(stages):
        if kind == 'bs':
            stages += [('r%d' % phase, layer, first + nt - 1 + SUM_STEPS[min(layer, 2)][phase]) for phase in range(5)]
    return stages, max(first + (1 if kind[0] in 'rm' else nt) for kind, _, first in stages)


def kernel(sizes, vol, cot, taps, w, b, out, gw_out, gb_out,
           vols, a1, a3, gp, grad, d3, d1, sb, second, yh, zh, zs, wt,
           mfx, mfy, mfyh, mfz, mbx, mby, mbz, mbzh, sel,
           gwx, rx, rq, sum_send, sum_recv,
           in_sem, cot_sem, out_sem, send_sem, recv_sem, xsend, xrecv):
    nx, ny, nz, num_layers, num_taps, by_len, bz_len = sizes
    half = (num_taps - 1) // 2
    planes = a1.shape[0]
    rows = by_len * bz_len
    edge_y = half * bz_len
    pairs = by_len // half
    edge = PLANES * half * half
    nt = planes // PLANES
    part_x = w.shape[1] // nx
    group = ny * nz
    part_q = part_x // group
    my_x, my_y, my_z = lax.axis_index('gx'), lax.axis_index('gy'), lax.axis_index('gz')
    y_lo, y_hi = my_y > 0, my_y < ny - 1
    z_lo, z_hi = my_z > 0, my_z < nz - 1
    x_peer = {'gx': 1 - my_x}

    def x_of(j):
        return my_x * j + (1 - my_x) * (planes - 1 - j)

    my_q = my_z * ny + my_y

    def chip(q):
        return {'gy': lax.rem(q, ny), 'gz': q // ny}

    barrier = pltpu.get_barrier_semaphore()
    pl.semaphore_signal(barrier, inc=1, device_id=x_peer, device_id_type=MESH)

    def signal_chip(offset, carry):
        pl.semaphore_signal(barrier, inc=1, device_id=chip(lax.rem(my_q + offset, group)), device_id_type=MESH)
        return carry

    lax.fori_loop(1, group, signal_chip, 0)

    def in_copy(j):
        return pltpu.make_async_copy(vol.at[x_of(j)], vols.at[0, j + half], in_sem.at[j])

    def cot_copy(j):
        return pltpu.make_async_copy(cot.at[x_of(j)], grad.at[j], cot_sem.at[j])

    def start_in(j, carry):
        in_copy(j).start()
        cot_copy(j).start()
        return carry

    lax.fori_loop(0, planes, start_in, 0)

    half_y, half_rows = by_len // 2, rows // 2

    def iota(shape, axis):
        return lax.broadcasted_iota(jnp.int32, shape, axis)

    def banded(layer, axis, back, hop, inside):
        total = jnp.zeros(hop.shape, F32)
        for t in range(num_taps):
            tap = taps[layer, axis, num_taps - 1 - t if back else t]
            if axis == 0:
                tap = jnp.where(my_x == 1, tap, taps[layer, axis, t if back else num_taps - 1 - t])
            total = jnp.where(hop == t, tap, total)
        return jnp.where(inside, total, 0.0).astype(BF16)

    def edge_index(e):
        return e // edge, e % edge // (half * half), e % (half * half) // half, e % half

    def grid(row_count, column_count):
        return iota((row_count, column_count), 0), iota((row_count, column_count), 1)

    def build_forward(layer, carry):
        i, k = grid(PLANES * edge_y, (PLANES + 2 * half) * edge_y)
        mfx[layer, :PLANES * edge_y] = banded(layer, 0, False, k // edge_y - i // edge_y, k % edge_y == i % edge_y)
        i, k = grid(2 * edge, (PLANES + 2 * half) * edge_y)
        side, plane, depth, y = edge_index(i)
        z = depth + side * (bz_len - half)
        mfx[layer, PLANES * edge_y:] = banded(layer, 0, False, k // edge_y - plane, k % edge_y == y * bz_len + z)
        i, k = grid(half_rows, half_rows + 2 * edge_y)
        mfy[layer] = banded(layer, 1, False, k // bz_len - i // bz_len, k % bz_len == i % bz_len)
        i, k = grid(PLANES * half * by_len, (pairs + 2) * edge)
        side, plane, depth, y = edge_index(k % edge)
        y = (k // edge - 1) * half + y
        i_y = i // (half * half_y) % 2 * half_y + i % half_y
        inside = (plane == i // (half * by_len)) & (depth == i // half_y % half)
        mfyh[layer] = banded(layer, 1, False, y - i_y + half, inside)
        i, k = grid(half_rows, half_rows)
        mfz[layer, :, :half_rows] = banded(layer, 2, False, k % bz_len - i % bz_len + half, k // bz_len == i // bz_len)
        i, k = grid(half_rows, half * by_len)
        hop = k // half_y % half + k // (half * half_y) * (bz_len + half) - i % bz_len
        mfz[layer, :, half_rows:] = banded(layer, 2, False, hop, k % half_y == i // bz_len)
        return carry

    def build_backward(layer, tau):
        i, k = grid(PLANES * edge_y, (PLANES + 2 * half) * edge_y)
        mbx[layer] = banded(layer, 0, True, k // edge_y - i // edge_y, k % edge_y == i % edge_y)
        i, k = grid(half_rows, half_rows + 2 * edge_y)
        mby[layer] = banded(layer, 1, True, k // bz_len - i // bz_len, k % bz_len == i % bz_len)
        i, k = grid(half_rows, half_rows)
        own_back = banded(layer, 2, True, k % bz_len - i % bz_len + half, k // bz_len == i // bz_len)
        i, k = grid(half_rows, pairs * edge)
        side, (_, plane, depth, y) = k // (pairs * edge // 2), edge_index(k % edge)
        y = k // edge % (pairs // 2) * half + y
        hop = depth + side * (bz_len + half) - i % bz_len
        for p in range(PLANES):
            mbz[layer, p, :, :half_rows] = own_back
            mbz[layer, p, :, half_rows:] = banded(layer, 2, True, hop, (y == i // bz_len) & (plane == p))
        i, k = grid(PLANES * edge_y, PLANES * edge_y)
        mbzh[layer, :, :PLANES * edge_y] = banded(layer, 2, True, k % bz_len - i % bz_len + half, k // bz_len == i // bz_len)
        i, k = grid(PLANES * edge_y, 2 * edge)
        side, plane, depth, y = edge_index(k)
        hop = depth + side * (bz_len + half) - i % bz_len
        mbzh[layer, :, PLANES * edge_y:] = banded(layer, 2, True, hop, (plane == i // edge_y) & (y == i // bz_len % half))
        wt[layer] = jnp.transpose(w[layer].astype(F32)).astype(BF16)

    lax.fori_loop(0, num_layers, build_forward, 0)
    i, k = grid(2 * edge, PLANES * edge_y)
    side, plane, depth, y = edge_index(i)
    z = depth + side * (bz_len - half)
    sel[...] = jnp.where((k // edge_y == plane) & (k % edge_y == y * bz_len + z), 1.0, 0.0).astype(BF16)

    for layer in range(num_layers):
        vols[layer, planes + half:] = jnp.zeros((half,) + vols.shape[2:], BF16)
        d1[layer, planes + half:] = jnp.zeros((half,) + d1.shape[2:], BF16)

    def zero_halo(where, clear):
        @pl.when(where)
        def _():
            def body(stage, carry):
                clear(stage)
                return carry
            lax.fori_loop(0, 2 * num_layers, body, 0)

    def clear_y(side):
        def clear(stage):
            yh[stage, :, side] = jnp.zeros(yh.shape[1:2] + yh.shape[3:], BF16)
            zh[stage, :, :, side * (pairs + 1)] = jnp.zeros(zh.shape[1:3] + zh.shape[4:], BF16)
        return clear

    def clear_z(side):
        def clear(stage):
            zh[stage, :, side] = jnp.zeros(zh.shape[1:2] + zh.shape[3:], BF16)
        return clear

    zero_halo(my_y == 0, clear_y(0))
    zero_halo(my_y == ny - 1, clear_y(1))
    zero_halo(my_z == 0, clear_z(0))
    zero_halo(my_z == nz - 1, clear_z(1))
    gwx[...] = jnp.zeros(gwx.shape, F32)

    pl.semaphore_wait(barrier, group)

    def exchange(src, stage, tau):
        at = pl.ds(tau * PLANES, PLANES)
        y_near, z_near = {0: None, 1: y_hi, -1: y_lo}, {0: None, 1: z_hi, -1: z_lo}
        entries = []
        for dy, dz in ((1, 0), (-1, 0), (0, 1), (0, -1), (1, 1), (1, -1), (-1, 1), (-1, -1)):
            device = {}
            if dy:
                device['gy'] = jnp.clip(my_y + dy, 0, ny - 1)
            if dz:
                device['gz'] = jnp.clip(my_z + dz, 0, nz - 1)
            if dz == 0:
                source = src.at[at, pl.ds(rows - edge_y if dy > 0 else 0, edge_y)]
                target = yh.at[stage, at, 0 if dy > 0 else 1]
            else:
                from_side, to_side = (1, 0) if dz > 0 else (0, 1)
                if dy == 0:
                    source, target = zs.at[stage, tau, from_side], zh.at[stage, tau, to_side, pl.ds(1, pairs)]
                else:
                    source = zs.at[stage, tau, from_side, pairs - 1 if dy > 0 else 0]
                    target = zh.at[stage, tau, to_side, 0 if dy > 0 else pairs + 1]
            copy = pltpu.make_async_remote_copy(
                src_ref=source, dst_ref=target, send_sem=send_sem.at[stage, tau, len(entries)],
                recv_sem=recv_sem.at[stage, tau, len(entries)], device_id=device, device_id_type=MESH)
            sends = [near for near in (y_near[dy], z_near[dz]) if near is not None]
            receives = [near for near in (y_near[-dy], z_near[-dz]) if near is not None]
            entries.append((copy, functools.reduce(jnp.logical_and, sends), functools.reduce(jnp.logical_and, receives)))
        return entries

    def start(entries):
        for copy, sends, _ in entries:
            pl.when(sends)(copy.start)

    def wait(entries):
        for copy, sends, receives in entries:
            pl.when(sends)(copy.wait_send)
            pl.when(receives)(copy.wait_recv)

    def x_copy(buf, stage, layer, j):
        src = vol.at[x_of(j)] if stage == 0 else buf.at[layer, half + j]
        return pltpu.make_async_remote_copy(
            src_ref=src, dst_ref=buf.at[layer, half - 1 - j],
            send_sem=xsend.at[stage, j], recv_sem=xrecv.at[stage, j], device_id=x_peer, device_id_type=MESH)

    def start_x(buf, stage, layer, tau):
        for task in range(-(-half // PLANES)):
            @pl.when(tau == task)
            def _():
                for j in range(task * PLANES, min(half, (task + 1) * PLANES)):
                    x_copy(buf, stage, layer, j).start()

    def wait_x(buf, stage, layer, tau):
        @pl.when(tau == 0)
        def _():
            for j in range(half):
                x_copy(buf, stage, layer, j).wait()

    for j in range(half):
        x_copy(vols, 0, 0, j).start()

    def wait_in(j, carry):
        in_copy(j).wait()
        return carry

    lax.fori_loop(0, planes, wait_in, 0)

    def x_source(buf, layer, tau, group):
        at = pl.ds(group * edge_y, edge_y)
        return jnp.concatenate([buf[layer, tau * PLANES + p, at, :] for p in range(PLANES + 2 * half)], axis=0)

    def fx(layer, tau):
        wait_x(vols, layer, layer, tau)
        for group in range(pairs):
            total = dot(mfx[layer], x_source(vols, layer, tau, group)).astype(BF16)
            for p in range(PLANES):
                a1[tau * PLANES + p, group * edge_y:(group + 1) * edge_y] = total[p * edge_y:(p + 1) * edge_y]
            for side in range(2):
                first = PLANES * edge_y + side * edge
                zs[layer, tau, side, group] = total[first:first + edge]
        start(exchange(a1, layer, tau))

    def fz(layer, tau):
        wait(exchange(a1, layer, tau))
        bias = b[layer, :][None, :]
        channels = w.shape[1]
        z_halo = [dot(mfyh[layer], zh[layer, tau, side].reshape((pairs + 2) * edge, channels)).astype(BF16) for side in range(2)]
        for p in range(PLANES):
            j = tau * PLANES + p
            for part in range(2):
                if part == 0:
                    source = jnp.concatenate([yh[layer, j, 0], a1[j, :half_rows + edge_y]], axis=0)
                else:
                    source = jnp.concatenate([a1[j, half_rows - edge_y:], yh[layer, j, 1]], axis=0)
                second[p, part] = dot(mfy[layer], source).astype(BF16)
        for p in range(PLANES):
            for part in range(2):
                size = half * half_y
                first = (p * 2 + part) * size
                source = jnp.concatenate([second[p, part]] + [halo[first:first + size] for halo in z_halo], axis=0)
                a3[layer, tau * PLANES + p, part * half_rows:(part + 1) * half_rows] = dot(mfz[layer], source).astype(BF16)
        for p in range(PLANES):
            j = tau * PLANES + p
            for part in range(2):
                pre = dot(a3[layer, j, part * half_rows:(part + 1) * half_rows], w[layer])
                for first in range(0, half_rows, CHUNK):
                    at = slice(part * half_rows + first, part * half_rows + first + CHUNK)
                    z = pre[first:first + CHUNK] + bias
                    cdf = 0.5 * lax.erf(z * SQRT_HALF) + 0.5
                    gp[layer, j, at] = cdf + z * (jnp.exp2((z * z) * -HALF_LOG2_E) * INV_SQRT_2PI)
                    if layer + 1 < num_layers:
                        vols[layer + 1, j + half, at] = (vols[layer, j + half, at].astype(F32) + z * cdf).astype(BF16)
        if layer + 1 < num_layers:
            start_x(vols, layer + 1, layer + 1, tau)

    def bs(layer, tau):
        stage = num_layers + layer
        channels = w.shape[1]
        if layer == num_layers - 1:
            for p in range(PLANES):
                cot_copy(tau * PLANES + p).wait()
        total_b = gwx[layer, 0, part_x:]
        for group in range(pairs):
            chunks = []
            for p in range(PLANES):
                j = tau * PLANES + p
                at = slice(group * edge_y, (group + 1) * edge_y)
                scaled = gp[layer, j, at] * grad[j, at].astype(F32)
                total_b = total_b + jnp.sum(scaled.reshape(edge_y // 8, 8, channels), axis=0)
                chunks.append(scaled.astype(BF16))
                sb[p, at] = chunks[-1]
            mixed = dot(jnp.concatenate(chunks, axis=0), wt[layer]).astype(BF16)
            for p in range(PLANES):
                d3[tau * PLANES + p, group * edge_y:(group + 1) * edge_y] = mixed[p * edge_y:(p + 1) * edge_y]
        for group in range(pairs):
            mixed = jnp.concatenate([d3[tau * PLANES + p, group * edge_y:(group + 1) * edge_y] for p in range(PLANES)], axis=0)
            edges = dot(sel[...], mixed).astype(BF16)
            for side in range(2):
                zs[stage, tau, side, group] = edges[side * edge:(side + 1) * edge]
        gwx[layer, 0, part_x:] = total_b
        start(exchange(d3, stage, tau))
        product = lax.dot_general(
            a3[layer, pl.ds(tau * PLANES, PLANES)].reshape(PLANES * rows, channels), sb[...].reshape(PLANES * rows, channels),
            (((0,), (0,)), ((), ())), preferred_element_type=F32)
        for side in range(nx):
            gwx[layer, side, :part_x] += product[side * part_x:(side + 1) * part_x]

    def by(layer, tau):
        stage = num_layers + layer
        channels = w.shape[1]
        wait(exchange(d3, stage, tau))
        y_halo = []
        for side in range(2):
            corner = side * (pairs + 1)
            source = jnp.concatenate(
                [yh[stage, tau * PLANES + p, side] for p in range(PLANES)] + [zh[stage, tau, z_side, corner] for z_side in range(2)], axis=0)
            y_halo.append(dot(mbzh[layer], source).astype(BF16))
        for p in range(PLANES):
            j = tau * PLANES + p
            for part in range(2):
                halves = [zh[stage, tau, side, pl.ds(1 + part * (pairs // 2), pairs // 2)] for side in range(2)]
                source = jnp.concatenate(
                    [d3[j, part * half_rows:(part + 1) * half_rows]] + [halo.reshape(pairs // 2 * edge, channels) for halo in halves], axis=0)
                second[p, part] = dot(mbz[layer, p], source).astype(BF16)
        for p in range(PLANES):
            j = tau * PLANES + p
            at = slice(p * edge_y, (p + 1) * edge_y)
            for part in range(2):
                if part == 0:
                    source = jnp.concatenate([y_halo[0][at], second[p, 0], second[p, 1, :edge_y]], axis=0)
                else:
                    source = jnp.concatenate([second[p, 0, half_rows - edge_y:], second[p, 1], y_halo[1][at]], axis=0)
                d1[layer, j + half, part * half_rows:(part + 1) * half_rows] = dot(mby[layer], source).astype(BF16)
        start_x(d1, stage, layer, tau)

    def out_copy(j):
        return pltpu.make_async_copy(grad.at[j], out.at[x_of(j)], out_sem.at[j])

    def bx(layer, tau):
        wait_x(d1, num_layers + layer, layer, tau)

        for group in range(pairs):
            at = slice(group * edge_y, (group + 1) * edge_y)
            total = dot(mbx[layer], x_source(d1, layer, tau, group))
            for p in range(PLANES):
                j = tau * PLANES + p
                grad[j, at] = (grad[j, at].astype(F32) + total[p * edge_y:(p + 1) * edge_y]).astype(BF16)
        if layer == 0:
            for p in range(PLANES):
                out_copy(tau * PLANES + p).start()

    def sum_copy(layer, phase, offset, src, dst, device):
        return pltpu.make_async_remote_copy(
            src_ref=src, dst_ref=dst, send_sem=sum_send.at[layer, phase, offset], recv_sem=sum_recv.at[layer, phase, offset],
            device_id=device, device_id_type=MESH)

    def core_copy(layer, phase):
        if phase == 0:
            return sum_copy(layer, 0, 0, gwx.at[layer, 1 - my_x], rx.at[layer], x_peer)
        at = pl.ds(pl.multiple_of(my_x * part_x, part_x), part_x)
        return sum_copy(layer, 3, 0, gw_out.at[layer, at], gw_out.at[layer, at], x_peer)

    def own_rows():
        return pl.ds(pl.multiple_of(my_x * part_x + my_q * part_q, part_q), part_q)

    def chip_copy(layer, phase, offset):
        other = lax.rem(my_q + offset, group)
        if phase == 1:
            return sum_copy(layer, 1, offset, rq.at[layer, 1, other], rq.at[layer, 0, my_q], chip(other))
        return sum_copy(layer, 2, offset, gw_out.at[layer, own_rows()], gw_out.at[layer, own_rows()], chip(other))

    def each_chip(layer, phase, act):
        def body(offset, carry):
            act(chip_copy(layer, phase, offset))
            return carry
        lax.fori_loop(1, group, body, 0)

    def r0(layer, tau):
        gwx[layer, 1, part_x:] = gwx[layer, 0, part_x:]
        core_copy(layer, 0).start()

    def r1(layer, tau):
        core_copy(layer, 0).wait()
        bias = gwx[layer, my_x, part_x:] + rx[layer, part_x:]
        for q in range(group):
            at = slice(q * part_q, (q + 1) * part_q)
            rq[layer, 1, q, :part_q] = gwx[layer, my_x, at] + rx[layer, at]
            rq[layer, 1, q, part_q:] = bias
        rq[layer, 0, my_q] = rq[layer, 1, my_q]
        each_chip(layer, 1, lambda copy: copy.start())

    def r2(layer, tau):
        each_chip(layer, 1, lambda copy: copy.wait())
        total = rq[layer, 0, 0]
        for q in range(1, group):
            total = total + rq[layer, 0, q]
        gw_out[layer, own_rows()] = total[:part_q]
        gb_out[layer, :] = jnp.sum(total[part_q:], axis=0)
        each_chip(layer, 2, lambda copy: copy.start())

    def r3(layer, tau):
        each_chip(layer, 2, lambda copy: copy.wait())
        core_copy(layer, 3).start()

    def r4(layer, tau):
        core_copy(layer, 3).wait()

    tasks = {'r0': r0, 'r1': r1, 'r2': r2, 'r3': r3, 'r4': r4, 'm': build_backward, 'fx': fx, 'fz': fz, 'bs': bs, 'by': by, 'bx': bx}
    stages, last = stage_list(num_layers, nt)

    def step(s, carry):
        for kind, layer, first in stages:
            tau = s - first

            @pl.when((tau >= 0) & (tau < (1 if kind[0] in 'rm' else nt)))
            def _():
                tasks[kind](layer, tau)
        return carry

    lax.fori_loop(0, last, step, 0)

    def wait_out(j, carry):
        out_copy(j).wait()
        return carry

    lax.fori_loop(0, planes, wait_out, 0)


def solution(mesh):
    names = ('gx', 'gy', 'gz')
    nx, ny, nz = (mesh.shape[axis_name] for axis_name in names)
    assert nx == 2
    vol_spec = P('dp', 'gx', 'gy', 'gz')

    def local_step(volume, cot_out, filter_taps, w_mix, b_mix):
        channels, planes, by_len, bz_len = volume.shape
        num_layers, _, num_taps = filter_taps.shape
        half = (num_taps - 1) // 2
        rows = by_len * bz_len
        edge_y, pairs, edge = half * bz_len, by_len // half, PLANES * half * half
        half_rows = rows // 2
        nt = planes // PLANES
        stages = 2 * num_layers
        part_x = channels // nx
        part_q = part_x // (ny * nz)

        def to_rows(block):
            return jnp.transpose(block, (1, 2, 3, 0)).reshape(planes, rows, channels)

        any_spec = pl.BlockSpec(memory_space=pl.ANY)
        vmem_spec = pl.BlockSpec(memory_space=pltpu.VMEM)
        smem_spec = pl.BlockSpec(memory_space=pltpu.SMEM)
        block = (planes, rows, channels)
        dma = pltpu.SemaphoreType.DMA
        grad_rows, grad_w, grad_b = pl.pallas_call(
            functools.partial(kernel, (nx, ny, nz, num_layers, num_taps, by_len, bz_len)),
            out_shape=(
                jax.ShapeDtypeStruct(block, BF16),
                jax.ShapeDtypeStruct((num_layers, channels, channels), F32),
                jax.ShapeDtypeStruct((num_layers, channels), F32),
            ),
            in_specs=[any_spec, any_spec, smem_spec, vmem_spec, vmem_spec],
            out_specs=(any_spec, vmem_spec, vmem_spec),
            scratch_shapes=[
                pltpu.VMEM((num_layers, planes + 2 * half, rows, channels), BF16),
                pltpu.VMEM(block, BF16),
                pltpu.VMEM((num_layers,) + block, BF16),
                pltpu.VMEM((num_layers,) + block, F32),
                pltpu.VMEM(block, BF16),
                pltpu.VMEM(block, BF16),
                pltpu.VMEM((num_layers, planes + 2 * half, rows, channels), BF16),
                pltpu.VMEM((PLANES, rows, channels), BF16),
                pltpu.VMEM((PLANES, 2, half_rows, channels), BF16),
                pltpu.VMEM((stages, planes, 2, edge_y, channels), BF16),
                pltpu.VMEM((stages, nt, 2, pairs + 2, edge, channels), BF16),
                pltpu.VMEM((stages, nt, 2, pairs, edge, channels), BF16),
                pltpu.VMEM((num_layers, channels, channels), BF16),
                pltpu.VMEM((num_layers, PLANES * edge_y + 2 * edge, (PLANES + 2 * half) * edge_y), BF16),
                pltpu.VMEM((num_layers, half_rows, half_rows + 2 * edge_y), BF16),
                pltpu.VMEM((num_layers, PLANES * half * by_len, (pairs + 2) * edge), BF16),
                pltpu.VMEM((num_layers, half_rows, half_rows + half * by_len), BF16),
                pltpu.VMEM((num_layers, PLANES * edge_y, (PLANES + 2 * half) * edge_y), BF16),
                pltpu.VMEM((num_layers, half_rows, half_rows + 2 * edge_y), BF16),
                pltpu.VMEM((num_layers, PLANES, half_rows, half_rows + pairs * edge), BF16),
                pltpu.VMEM((num_layers, PLANES * edge_y, PLANES * edge_y + 2 * edge), BF16),
                pltpu.VMEM((2 * edge, PLANES * edge_y), BF16),
                pltpu.VMEM((num_layers, nx, part_x + 8, channels), F32),
                pltpu.VMEM((num_layers, part_x + 8, channels), F32),
                pltpu.VMEM((num_layers, 2, ny * nz, part_q + 8, channels), F32),
                dma((num_layers, 4, ny * nz)), dma((num_layers, 4, ny * nz)),
                dma((planes,)), dma((planes,)), dma((planes,)),
                dma((stages, nt, 8)), dma((stages, nt, 8)),
                dma((stages, half)), dma((stages, half)),
            ],
            compiler_params=pltpu.CompilerParams(
                collective_id=0, has_side_effects=True, vmem_limit_bytes=64000 * 1024),
            name='stack',
        )(to_rows(volume), to_rows(cot_out), filter_taps, w_mix, b_mix)
        grad_volume = jnp.transpose(grad_rows.reshape(planes, by_len, bz_len, channels), (3, 0, 1, 2))
        return grad_volume, grad_w, grad_b

    return jax.shard_map(local_step, mesh=mesh, in_specs=(vol_spec, vol_spec, P(), P(), P()), out_specs=(vol_spec, P('dp'), P('dp')), check_vma=False)
```

time: 110 us -> 89.9 us (0.82)
  Pallas kernels: 105 us -> 84.5 us
    pallas_call x1, Pallas kernels: 105 us -> 84.5 us  [local_step(): pl.pallas_call(functools.partial(kernel, (nx, ny, nz, num_layers, num_tap...]
where the time goes in v6:
time: 89.9 us; the launch traced here: 89.8 us
  Pallas kernels  84.5 us (94%)
  local copies, waits for them, and re-layouts  4.65 us (5%)
    pallas_call x1, Pallas kernels, local_step(): pl.pallas_call(functools.partial(kernel, (nx, ny, nz, num_layers, num_tap...  84.5 us
    unnamed x7, local copies, waits for them, and re-layouts  4.65 us

profile of v6, /device:TPU:97, one launch (start us, length us, event | category | flops | bytes accessed | tf_op | source)
XLA Modules:
  0.0 89.8 jit_solution(16446316510810070025)
XLA Ops:
  0.6 84.5 %stack.1 = (bf16[16,256,256]{2,1,0:T(8,128)(2,1)}, f32[3,256,256]{2,1,0:T(8,128)}, f32[3,256]{1,0:T(4,128)}) custom-call(bf16[16,256,256]{2,1,0:T(8,128)(2,1)} %bitcast.9, bf16[16,256,256]{2,1,0:T(8,128)(2,1)} %bitcast.10, f32[3,3,5]{2,1,0:T(4,128)} %taps.1, bf16[3,256,256]{2,1,0:T(8,128)(2,1)} %w.1, f32[3,256]{1,0:T(4,128)} %b.1), custom_call_target="tpu_custom_call" | custom-call | tf_op jit(solution)/shard_map/stack/pallas_call | solution.py:490
  85.1 0.0 copy-start
  85.1 0.0 copy-start.1
  85.1 3.2 %copy.11 = bf16[256,16,16,16]{0,3,2,1:T(8,128)(2,1)} copy(bf16[256,16,16,16]{0,3,2,1:T(8,128)(2,1)} %bitcast.11) | data formatting | bytes 4194304
  88.3 0.0 copy-done
  88.3 0.9 copy.12
  89.2 0.0 copy-done.1
  89.2 0.6 copy.13
Async XLA Ops:
  85.1 3.2 %copy-start = (f32[3,256,256]{2,1,0:T(8,128)S(1)}, f32[3,256,256]{2,1,0:T(8,128)}, u32[]{:S(2)}) copy-start(f32[3,256,256]{2,1,0:T(8,128)} %get-tuple-element.13) | copy-start | bytes 2359300
  85.1 4.1 %copy-start.1 = (f32[3,256]{1,0:T(4,128)S(1)}, f32[3,256]{1,0:T(4,128)}, u32[]{:S(2)}) copy-start(f32[3,256]{1,0:T(4,128)} %get-tuple-element.14) | copy-start | bytes 9220

commit v7 on v6

--- a/solution.py
+++ b/solution.py
@@ -9,8 +9,8 @@
 
 MESH = pl.DeviceIdType.MESH
 PLANES = 4
-LAG = 2
-SUM_STEPS = ((0, 1, 2, 3, 4), (0, 2, 5, 7, 8), (0, 2, 5, 7, 9))
+LAG = 3
+SUM_STEPS = ((0, 1, 3, 5, 6), (0, 2, 6, 9, 10), (0, 2, 6, 9, 10))
 XLAG = 1
 F32 = jnp.float32
 BF16 = jnp.bfloat16
@@ -43,11 +43,11 @@
     return stages, max(first + (1 if kind[0] in 'rm' else nt) for kind, _, first in stages)
 
 
-def kernel(sizes, vol, cot, taps, w, b, out, gw_out, gb_out,
-           vols, a1, a3, gp, grad, d3, d1, sb, second, yh, zh, zs, wt,
+def kernel(sizes, vol, cot, taps, w, b, grad, gw_out, gb_out,
+           vols, a1, a3, gp, d3, d1, sb, second, yh, zh, zs, wt,
            mfx, mfy, mfyh, mfz, mbx, mby, mbz, mbzh, sel,
-           gwx, rx, rq, sum_send, sum_recv,
-           in_sem, cot_sem, out_sem, send_sem, recv_sem, xsend, xrecv):
+           gwx, gb_acc, rx, rq, sum_send, sum_recv,
+           in_sem, cot_sem, send_sem, recv_sem, xsend, xrecv):
     nx, ny, nz, num_layers, num_taps, by_len, bz_len = sizes
     half = (num_taps - 1) // 2
     planes = a1.shape[0]
@@ -84,15 +84,14 @@
     def in_copy(j):
         return pltpu.make_async_copy(vol.at[x_of(j)], vols.at[0, j + half], in_sem.at[j])
 
-    def cot_copy(j):
-        return pltpu.make_async_copy(cot.at[x_of(j)], grad.at[j], cot_sem.at[j])
+    cot_copy = pltpu.make_async_copy(cot, grad, cot_sem)
 
     def start_in(j, carry):
         in_copy(j).start()
-        cot_copy(j).start()
         return carry
 
     lax.fori_loop(0, planes, start_in, 0)
+    cot_copy.start()
 
     half_y, half_rows = by_len // 2, rows // 2
 
@@ -192,6 +191,7 @@
     zero_halo(my_z == 0, clear_z(0))
     zero_halo(my_z == nz - 1, clear_z(1))
     gwx[...] = jnp.zeros(gwx.shape, F32)
+    gb_acc[...] = jnp.zeros(gb_acc.shape, F32)
 
     pl.semaphore_wait(barrier, group)
 
@@ -312,15 +312,14 @@
         stage = num_layers + layer
         channels = w.shape[1]
         if layer == num_layers - 1:
-            for p in range(PLANES):
-                cot_copy(tau * PLANES + p).wait()
-        total_b = gwx[layer, 0, part_x:]
+            pl.when(tau == 0)(cot_copy.wait)
+        total_b = gb_acc[layer]
         for group in range(pairs):
             chunks = []
             for p in range(PLANES):
                 j = tau * PLANES + p
                 at = slice(group * edge_y, (group + 1) * edge_y)
-                scaled = gp[layer, j, at] * grad[j, at].astype(F32)
+                scaled = gp[layer, j, at] * grad[x_of(j), at].astype(F32)
                 total_b = total_b + jnp.sum(scaled.reshape(edge_y // 8, 8, channels), axis=0)
                 chunks.append(scaled.astype(BF16))
                 sb[p, at] = chunks[-1]
@@ -332,7 +331,7 @@
             edges = dot(sel[...], mixed).astype(BF16)
             for side in range(2):
                 zs[stage, tau, side, group] = edges[side * edge:(side + 1) * edge]
-        gwx[layer, 0, part_x:] = total_b
+        gb_acc[layer] = total_b
         start(exchange(d3, stage, tau))
         product = lax.dot_general(
             a3[layer, pl.ds(tau * PLANES, PLANES)].reshape(PLANES * rows, channels), sb[...].reshape(PLANES * rows, channels),
@@ -368,9 +367,6 @@
                 d1[layer, j + half, part * half_rows:(part + 1) * half_rows] = dot(mby[layer], source).astype(BF16)
         start_x(d1, stage, layer, tau)
 
-    def out_copy(j):
-        return pltpu.make_async_copy(grad.at[j], out.at[x_of(j)], out_sem.at[j])
-
     def bx(layer, tau):
         wait_x(d1, num_layers + layer, layer, tau)
 
@@ -378,20 +374,20 @@
             at = slice(group * edge_y, (group + 1) * edge_y)
             total = dot(mbx[layer], x_source(d1, layer, tau, group))
             for p in range(PLANES):
-                j = tau * PLANES + p
-                grad[j, at] = (grad[j, at].astype(F32) + total[p * edge_y:(p + 1) * edge_y]).astype(BF16)
-        if layer == 0:
-            for p in range(PLANES):
-                out_copy(tau * PLANES + p).start()
-
+                x = x_of(tau * PLANES + p)
+                grad[x, at] = (grad[x, at].astype(F32) + total[p * edge_y:(p + 1) * edge_y]).astype(BF16)
     def sum_copy(layer, phase, offset, src, dst, device):
         return pltpu.make_async_remote_copy(
             src_ref=src, dst_ref=dst, send_sem=sum_send.at[layer, phase, offset], recv_sem=sum_recv.at[layer, phase, offset],
             device_id=device, device_id_type=MESH)
 
+    def bias_rows(layer):
+        return 0 if layer else 8
+
     def core_copy(layer, phase):
         if phase == 0:
-            return sum_copy(layer, 0, 0, gwx.at[layer, 1 - my_x], rx.at[layer], x_peer)
+            at = pl.ds(0, part_x + bias_rows(layer))
+            return sum_copy(layer, 0, 0, gwx.at[layer, 1 - my_x, at], rx.at[layer, at], x_peer)
         at = pl.ds(pl.multiple_of(my_x * part_x, part_x), part_x)
         return sum_copy(layer, 3, 0, gw_out.at[layer, at], gw_out.at[layer, at], x_peer)
 
@@ -401,7 +397,8 @@
     def chip_copy(layer, phase, offset):
         other = lax.rem(my_q + offset, group)
         if phase == 1:
-            return sum_copy(layer, 1, offset, rq.at[layer, 1, other], rq.at[layer, 0, my_q], chip(other))
+            at = pl.ds(0, part_q + bias_rows(layer))
+            return sum_copy(layer, 1, offset, rq.at[layer, 1, other, at], rq.at[layer, 0, my_q, at], chip(other))
         return sum_copy(layer, 2, offset, gw_out.at[layer, own_rows()], gw_out.at[layer, own_rows()], chip(other))
 
     def each_chip(layer, phase, act):
@@ -411,26 +408,32 @@
         lax.fori_loop(1, group, body, 0)
 
     def r0(layer, tau):
-        gwx[layer, 1, part_x:] = gwx[layer, 0, part_x:]
+        if bias_rows(layer):
+            for side in range(nx):
+                for row in range(num_layers):
+                    gwx[layer, side, part_x + row, :] = jnp.sum(gb_acc[row], axis=0)
         core_copy(layer, 0).start()
 
     def r1(layer, tau):
         core_copy(layer, 0).wait()
-        bias = gwx[layer, my_x, part_x:] + rx[layer, part_x:]
+        extra = bias_rows(layer)
         for q in range(group):
             at = slice(q * part_q, (q + 1) * part_q)
             rq[layer, 1, q, :part_q] = gwx[layer, my_x, at] + rx[layer, at]
-            rq[layer, 1, q, part_q:] = bias
-        rq[layer, 0, my_q] = rq[layer, 1, my_q]
+            if extra:
+                rq[layer, 1, q, part_q:] = gwx[layer, my_x, part_x:] + rx[layer, part_x:]
+        rq[layer, 0, my_q, :part_q + extra] = rq[layer, 1, my_q, :part_q + extra]
         each_chip(layer, 1, lambda copy: copy.start())
 
     def r2(layer, tau):
         each_chip(layer, 1, lambda copy: copy.wait())
-        total = rq[layer, 0, 0]
+        count = part_q + bias_rows(layer)
+        total = rq[layer, 0, 0, :count]
         for q in range(1, group):
-            total = total + rq[layer, 0, q]
+            total = total + rq[layer, 0, q, :count]
         gw_out[layer, own_rows()] = total[:part_q]
-        gb_out[layer, :] = jnp.sum(total[part_q:], axis=0)
+        if bias_rows(layer):
+            gb_out[...] = total[part_q:part_q + num_layers]
         each_chip(layer, 2, lambda copy: copy.start())
 
     def r3(layer, tau):
@@ -453,12 +456,6 @@
         return carry
 
     lax.fori_loop(0, last, step, 0)
-
-    def wait_out(j, carry):
-        out_copy(j).wait()
-        return carry
-
-    lax.fori_loop(0, planes, wait_out, 0)
 
 
 def solution(mesh):
@@ -490,18 +487,17 @@
         grad_rows, grad_w, grad_b = pl.pallas_call(
             functools.partial(kernel, (nx, ny, nz, num_layers, num_taps, by_len, bz_len)),
             out_shape=(
-                jax.ShapeDtypeStruct(block, BF16),
-                jax.ShapeDtypeStruct((num_layers, channels, channels), F32),
-                jax.ShapeDtypeStruct((num_layers, channels), F32),
+                pltpu.VMEM(block, BF16),
+                pltpu.VMEM((num_layers, channels, channels), F32),
+                pltpu.VMEM((num_layers, channels), F32),
             ),
             in_specs=[any_spec, any_spec, smem_spec, vmem_spec, vmem_spec],
-            out_specs=(any_spec, vmem_spec, vmem_spec),
+            out_specs=(vmem_spec, vmem_spec, vmem_spec),
             scratch_shapes=[
                 pltpu.VMEM((num_layers, planes + 2 * half, rows, channels), BF16),
                 pltpu.VMEM(block, BF16),
                 pltpu.VMEM((num_layers,) + block, BF16),
                 pltpu.VMEM((num_layers,) + block, F32),
-                pltpu.VMEM(block, BF16),
                 pltpu.VMEM(block, BF16),
                 pltpu.VMEM((num_layers, planes + 2 * half, rows, channels), BF16),
                 pltpu.VMEM((PLANES, rows, channels), BF16),
@@ -520,15 +516,16 @@
                 pltpu.VMEM((num_layers, PLANES * edge_y, PLANES * edge_y + 2 * edge), BF16),
                 pltpu.VMEM((2 * edge, PLANES * edge_y), BF16),
                 pltpu.VMEM((num_layers, nx, part_x + 8, channels), F32),
+                pltpu.VMEM((num_layers, 8, channels), F32),
                 pltpu.VMEM((num_layers, part_x + 8, channels), F32),
                 pltpu.VMEM((num_layers, 2, ny * nz, part_q + 8, channels), F32),
                 dma((num_layers, 4, ny * nz)), dma((num_layers, 4, ny * nz)),
-                dma((planes,)), dma((planes,)), dma((planes,)),
+                dma((planes,)), dma,
                 dma((stages, nt, 8)), dma((stages, nt, 8)),
                 dma((stages, half)), dma((stages, half)),
             ],
             compiler_params=pltpu.CompilerParams(
-                collective_id=0, has_side_effects=True, vmem_limit_bytes=64000 * 1024),
+                collective_id=0, has_side_effects=True, vmem_limit_bytes=59000 * 1024),
             name='stack',
         )(to_rows(volume), to_rows(cot_out), filter_taps, w_mix, b_mix)
         grad_volume = jnp.transpose(grad_rows.reshape(planes, by_len, bz_len, channels), (3, 0, 1, 2))

time: 89.9 us -> 85 us (0.945)
  Pallas kernels: 84.5 us -> 81.4 us
  local copies, waits for them, and re-layouts: 4.65 us -> 2.79 us
    pallas_call x1, Pallas kernels: 84.5 us -> 81.4 us  [local_step(): pl.pallas_call(functools.partial(kernel, (nx, ny, nz, num_layers, num_tap...]
    unnamed x7 -> x3, local copies, waits for them, and re-layouts: 4.65 us -> 2.79 us
where the time goes in v7:
time: 85 us; the launch traced here: 84.9 us
  Pallas kernels  81.4 us (96%)
  local copies, waits for them, and re-layouts  2.79 us (3%)
    pallas_call x1, Pallas kernels, local_step(): pl.pallas_call(functools.partial(kernel, (nx, ny, nz, num_layers, num_tap...  81.4 us
    unnamed x3, local copies, waits for them, and re-layouts  2.79 us

profile of v7, /device:TPU:97, one launch (start us, length us, event | category | flops | bytes accessed | tf_op | source)
XLA Modules:
  0.0 84.9 jit_solution(5314454501887887387)
XLA Ops:
  0.6 81.4 %stack.1 = (bf16[16,256,256]{2,1,0:T(8,128)(2,1)S(1)}, f32[3,256,256]{2,1,0:T(8,128)S(1)}, f32[3,256]{1,0:T(4,128)S(1)}) custom-call(bf16[16,256,256]{2,1,0:T(8,128)(2,1)} %bitcast.10, bf16[16,256,256]{2,1,0:T(8,128)(2,1)} %bitcast.11, f32[3,3,5]{2,1,0:T(4,128)} %taps.1, bf16[3,256,256]{2,1,0:T(8,128)(2,1)} %w.1, f32[3,256]{1,0:T(4,128)} %b.1), custom_call_target="tpu_custom_call" | custom-call | tf_op jit(solution)/shard_map/stack/pallas_call | solution.py:487
  82.1 1.3 %copy.11 = bf16[256,16,16,16]{0,3,2,1:T(8,128)(2,1)} copy(bf16[256,16,16,16]{0,3,2,1:T(8,128)(2,1)S(1)} %bitcast.9) | data formatting | bytes 4194304
  83.4 0.6 copy.13
  84.0 0.9 %copy.12 = f32[3,256,256]{2,1,0:T(8,128)} copy(f32[3,256,256]{2,1,0:T(8,128)S(1)} %get-tuple-element.10) | data formatting | bytes 1572864

commit v8 on v7

--- a/solution.py
+++ b/solution.py
@@ -9,8 +9,9 @@
 
 MESH = pl.DeviceIdType.MESH
 PLANES = 4
+LAST_LAG = 4
 LAG = 3
-SUM_STEPS = ((0, 1, 3, 5, 6), (0, 2, 6, 9, 10), (0, 2, 6, 9, 10))
+SUM_STEPS = ((0, 0, 4, 7, 9), (0, 2, 6, 10, 11), (0, 2, 9, 13, 15))
 XLAG = 1
 F32 = jnp.float32
 BF16 = jnp.bfloat16
@@ -33,9 +34,10 @@
         start += LAG + (XLAG if layer + 1 < num_layers else 0)
     for layer in reversed(range(num_layers)):
         stages.append(('bs', layer, start))
-        stages.append(('by', layer, start + LAG))
-        stages.append(('bx', layer, start + LAG + XLAG))
-        start += LAG + XLAG
+        lag = LAG if layer else LAST_LAG
+        stages.append(('by', layer, start + lag))
+        stages.append(('bx', layer, start + lag + XLAG))
+        start += lag + XLAG
     stages[1:1] = [('m', layer, layer) for layer in range(num_layers)]
     for kind, layer, first in list(stages):
         if kind == 'bs':
@@ -69,17 +71,14 @@
 
     my_q = my_z * ny + my_y
 
-    def chip(q):
-        return {'gy': lax.rem(q, ny), 'gz': q // ny}
+    other_y = [lax.rem(my_y + offset, ny) for offset in range(ny)]
+    other_z = [lax.rem(my_z + offset, nz) for offset in range(nz)]
+    others = [(y, z) for z in range(nz) for y in range(ny)][1:]
 
     barrier = pltpu.get_barrier_semaphore()
     pl.semaphore_signal(barrier, inc=1, device_id=x_peer, device_id_type=MESH)
-
-    def signal_chip(offset, carry):
-        pl.semaphore_signal(barrier, inc=1, device_id=chip(lax.rem(my_q + offset, group)), device_id_type=MESH)
-        return carry
-
-    lax.fori_loop(1, group, signal_chip, 0)
+    for y, z in others:
+        pl.semaphore_signal(barrier, inc=1, device_id={'gy': other_y[y], 'gz': other_z[z]}, device_id_type=MESH)
 
     def in_copy(j):
         return pltpu.make_async_copy(vol.at[x_of(j)], vols.at[0, j + half], in_sem.at[j])
@@ -162,36 +161,6 @@
     side, plane, depth, y = edge_index(i)
     z = depth + side * (bz_len - half)
     sel[...] = jnp.where((k // edge_y == plane) & (k % edge_y == y * bz_len + z), 1.0, 0.0).astype(BF16)
-
-    for layer in range(num_layers):
-        vols[layer, planes + half:] = jnp.zeros((half,) + vols.shape[2:], BF16)
-        d1[layer, planes + half:] = jnp.zeros((half,) + d1.shape[2:], BF16)
-
-    def zero_halo(where, clear):
-        @pl.when(where)
-        def _():
-            def body(stage, carry):
-                clear(stage)
-                return carry
-            lax.fori_loop(0, 2 * num_layers, body, 0)
-
-    def clear_y(side):
-        def clear(stage):
-            yh[stage, :, side] = jnp.zeros(yh.shape[1:2] + yh.shape[3:], BF16)
-            zh[stage, :, :, side * (pairs + 1)] = jnp.zeros(zh.shape[1:3] + zh.shape[4:], BF16)
-        return clear
-
-    def clear_z(side):
-        def clear(stage):
-            zh[stage, :, side] = jnp.zeros(zh.shape[1:2] + zh.shape[3:], BF16)
-        return clear
-
-    zero_halo(my_y == 0, clear_y(0))
-    zero_halo(my_y == ny - 1, clear_y(1))
-    zero_halo(my_z == 0, clear_z(0))
-    zero_halo(my_z == nz - 1, clear_z(1))
-    gwx[...] = jnp.zeros(gwx.shape, F32)
-    gb_acc[...] = jnp.zeros(gb_acc.shape, F32)
 
     pl.semaphore_wait(barrier, group)
 
@@ -253,6 +222,36 @@
 
     for j in range(half):
         x_copy(vols, 0, 0, j).start()
+
+    for layer in range(num_layers):
+        vols[layer, planes + half:] = jnp.zeros((half,) + vols.shape[2:], BF16)
+        d1[layer, planes + half:] = jnp.zeros((half,) + d1.shape[2:], BF16)
+
+    def zero_halo(where, clear):
+        @pl.when(where)
+        def _():
+            def body(stage, carry):
+                clear(stage)
+                return carry
+            lax.fori_loop(0, 2 * num_layers, body, 0)
+
+    def clear_y(side):
+        def clear(stage):
+            yh[stage, :, side] = jnp.zeros(yh.shape[1:2] + yh.shape[3:], BF16)
+            zh[stage, :, :, side * (pairs + 1)] = jnp.zeros(zh.shape[1:3] + zh.shape[4:], BF16)
+        return clear
+
+    def clear_z(side):
+        def clear(stage):
+            zh[stage, :, side] = jnp.zeros(zh.shape[1:2] + zh.shape[3:], BF16)
+        return clear
+
+    zero_halo(my_y == 0, clear_y(0))
+    zero_halo(my_y == ny - 1, clear_y(1))
+    zero_halo(my_z == 0, clear_z(0))
+    zero_halo(my_z == nz - 1, clear_z(1))
+    gwx[...] = jnp.zeros(gwx.shape, F32)
+    gb_acc[...] = jnp.zeros(gb_acc.shape, F32)
 
     def wait_in(j, carry):
         in_copy(j).wait()
@@ -395,17 +394,17 @@
         return pl.ds(pl.multiple_of(my_x * part_x + my_q * part_q, part_q), part_q)
 
     def chip_copy(layer, phase, offset):
-        other = lax.rem(my_q + offset, group)
+        y, z = others[offset]
+        device = {'gy': other_y[y], 'gz': other_z[z]}
         if phase == 1:
             at = pl.ds(0, part_q + bias_rows(layer))
-            return sum_copy(layer, 1, offset, rq.at[layer, 1, other, at], rq.at[layer, 0, my_q, at], chip(other))
-        return sum_copy(layer, 2, offset, gw_out.at[layer, own_rows()], gw_out.at[layer, own_rows()], chip(other))
+            source = rq.at[layer, 1, other_z[z] * ny + other_y[y], at]
+            return sum_copy(layer, 1, offset, source, rq.at[layer, 0, my_q, at], device)
+        return sum_copy(layer, 2, offset, gw_out.at[layer, own_rows()], gw_out.at[layer, own_rows()], device)
 
     def each_chip(layer, phase, act):
-        def body(offset, carry):
+        for offset in range(group - 1):
             act(chip_copy(layer, phase, offset))
-            return carry
-        lax.fori_loop(1, group, body, 0)
 
     def r0(layer, tau):
         if bias_rows(layer):
@@ -456,6 +455,17 @@
         return carry
 
     lax.fori_loop(0, last, step, 0)
+
+
+def write_kernel(count, grad, gw, gb, grad_out, gw_out, gb_out, sems):
+    part = grad.shape[0] // count
+    copies = [pltpu.make_async_copy(grad.at[pl.ds(k * part, part)], grad_out.at[pl.ds(k * part, part)], sems.at[k]) for k in range(count)]
+    copies += [pltpu.make_async_copy(gw.at[k], gw_out.at[k], sems.at[count + k]) for k in range(gw.shape[0])]
+    copies.append(pltpu.make_async_copy(gb, gb_out, sems.at[count + gw.shape[0]]))
+    for copy in copies:
+        copy.start()
+    for copy in copies:
+        copy.wait()
 
 
 def solution(mesh):
@@ -528,6 +538,20 @@
                 collective_id=0, has_side_effects=True, vmem_limit_bytes=59000 * 1024),
             name='stack',
         )(to_rows(volume), to_rows(cot_out), filter_taps, w_mix, b_mix)
+        count = 4
+        grad_rows, grad_w, grad_b = pl.pallas_call(
+            functools.partial(write_kernel, count),
+            out_shape=(
+                jax.ShapeDtypeStruct(block, BF16),
+                jax.ShapeDtypeStruct((num_layers, channels, channels), F32),
+                jax.ShapeDtypeStruct((num_layers, channels), F32),
+            ),
+            in_specs=[vmem_spec] * 3,
+            out_specs=(any_spec,) * 3,
+            scratch_shapes=[dma((count + num_layers + 1,))],
+            compiler_params=pltpu.CompilerParams(vmem_limit_bytes=1024 * 1024),
+            name='write',
+        )(*(pltpu.with_memory_space_constraint(value, pltpu.VMEM) for value in (grad_rows, grad_w, grad_b)))
         grad_volume = jnp.transpose(grad_rows.reshape(planes, by_len, bz_len, channels), (3, 0, 1, 2))
         return grad_volume, grad_w, grad_b
 

time: 85 us -> 83.2 us (0.979)
  local copies, waits for them, and re-layouts: 2.79 us -> 0 us
  Pallas kernels: 81.4 us -> 82.4 us
    unnamed x3 -> x0, local copies, waits for them, and re-layouts: 2.79 us -> none
    pallas_call x0 -> x1, Pallas kernels: none -> 1.64 us  [local_step(): pl.pallas_call(functools.partial(write_kernel, count), out_shape=(jax.Sha...]
where the time goes in v8:
time: 83.2 us; the launch traced here: 83.1 us
  Pallas kernels  82.4 us (99%)
    pallas_call x1, Pallas kernels, local_step(): pl.pallas_call(functools.partial(kernel, (nx, ny, nz, num_layers, num_tap...  80.8 us

profile of v8, /device:TPU:97, one launch (start us, length us, event | category | flops | bytes accessed | tf_op | source)
XLA Modules:
  0.0 83.1 jit_solution(14449899203032776593)
XLA Ops:
  0.6 80.8 %stack.1 = (bf16[16,256,256]{2,1,0:T(8,128)(2,1)S(1)}, f32[3,256,256]{2,1,0:T(8,128)S(1)}, f32[3,256]{1,0:T(4,128)S(1)}) custom-call(bf16[16,256,256]{2,1,0:T(8,128)(2,1)} %bitcast.9, bf16[16,256,256]{2,1,0:T(8,128)(2,1)} %bitcast.10, f32[3,3,5]{2,1,0:T(4,128)} %taps.1, bf16[3,256,256]{2,1,0:T(8,128)(2,1)} %w.1, f32[3,256]{1,0:T(4,128)} %b.1), custom_call_target="tpu_custom_call" | custom-call | tf_op jit(solution)/shard_map/stack/pallas_call | solution.py:497
  81.4 1.6 %write.1 = (bf16[16,256,256]{2,1,0:T(8,128)(2,1)}, f32[3,256,256]{2,1,0:T(8,128)}, f32[3,256]{1,0:T(4,128)}) custom-call(bf16[16,256,256]{2,1,0:T(8,128)(2,1)S(1)} %get-tuple-element.9.grad, f32[3,256,256]{2,1,0:T(8,128)S(1)} %get-tuple-element.10.gw, f32[3,256]{1,0:T(4,128)S(1)} %get-tuple-element.11.gb), custom_call_target="tpu_custom_call" | custom-call | tf_op jit(solution)/shard_map/write/pallas_call | solution.py:542

commit v9 on v8

--- a/solution.py
+++ b/solution.py
@@ -55,6 +55,7 @@
     planes = a1.shape[0]
     rows = by_len * bz_len
     edge_y = half * bz_len
+    half_y, half_rows = by_len // 2, rows // 2
     pairs = by_len // half
     edge = PLANES * half * half
     nt = planes // PLANES
@@ -92,83 +93,13 @@
     lax.fori_loop(0, planes, start_in, 0)
     cot_copy.start()
 
-    half_y, half_rows = by_len // 2, rows // 2
-
-    def iota(shape, axis):
-        return lax.broadcasted_iota(jnp.int32, shape, axis)
-
-    def banded(layer, axis, back, hop, inside):
-        total = jnp.zeros(hop.shape, F32)
-        for t in range(num_taps):
-            tap = taps[layer, axis, num_taps - 1 - t if back else t]
-            if axis == 0:
-                tap = jnp.where(my_x == 1, tap, taps[layer, axis, t if back else num_taps - 1 - t])
-            total = jnp.where(hop == t, tap, total)
-        return jnp.where(inside, total, 0.0).astype(BF16)
-
-    def edge_index(e):
-        return e // edge, e % edge // (half * half), e % (half * half) // half, e % half
-
-    def grid(row_count, column_count):
-        return iota((row_count, column_count), 0), iota((row_count, column_count), 1)
-
-    def build_forward(layer, carry):
-        i, k = grid(PLANES * edge_y, (PLANES + 2 * half) * edge_y)
-        mfx[layer, :PLANES * edge_y] = banded(layer, 0, False, k // edge_y - i // edge_y, k % edge_y == i % edge_y)
-        i, k = grid(2 * edge, (PLANES + 2 * half) * edge_y)
-        side, plane, depth, y = edge_index(i)
-        z = depth + side * (bz_len - half)
-        mfx[layer, PLANES * edge_y:] = banded(layer, 0, False, k // edge_y - plane, k % edge_y == y * bz_len + z)
-        i, k = grid(half_rows, half_rows + 2 * edge_y)
-        mfy[layer] = banded(layer, 1, False, k // bz_len - i // bz_len, k % bz_len == i % bz_len)
-        i, k = grid(PLANES * half * by_len, (pairs + 2) * edge)
-        side, plane, depth, y = edge_index(k % edge)
-        y = (k // edge - 1) * half + y
-        i_y = i // (half * half_y) % 2 * half_y + i % half_y
-        inside = (plane == i // (half * by_len)) & (depth == i // half_y % half)
-        mfyh[layer] = banded(layer, 1, False, y - i_y + half, inside)
-        i, k = grid(half_rows, half_rows)
-        mfz[layer, :, :half_rows] = banded(layer, 2, False, k % bz_len - i % bz_len + half, k // bz_len == i // bz_len)
-        i, k = grid(half_rows, half * by_len)
-        hop = k // half_y % half + k // (half * half_y) * (bz_len + half) - i % bz_len
-        mfz[layer, :, half_rows:] = banded(layer, 2, False, hop, k % half_y == i // bz_len)
-        return carry
-
-    def build_backward(layer, tau):
-        i, k = grid(PLANES * edge_y, (PLANES + 2 * half) * edge_y)
-        mbx[layer] = banded(layer, 0, True, k // edge_y - i // edge_y, k % edge_y == i % edge_y)
-        i, k = grid(half_rows, half_rows + 2 * edge_y)
-        mby[layer] = banded(layer, 1, True, k // bz_len - i // bz_len, k % bz_len == i % bz_len)
-        i, k = grid(half_rows, half_rows)
-        own_back = banded(layer, 2, True, k % bz_len - i % bz_len + half, k // bz_len == i // bz_len)
-        i, k = grid(half_rows, pairs * edge)
-        side, (_, plane, depth, y) = k // (pairs * edge // 2), edge_index(k % edge)
-        y = k // edge % (pairs // 2) * half + y
-        hop = depth + side * (bz_len + half) - i % bz_len
-        for p in range(PLANES):
-            mbz[layer, p, :, :half_rows] = own_back
-            mbz[layer, p, :, half_rows:] = banded(layer, 2, True, hop, (y == i // bz_len) & (plane == p))
-        i, k = grid(PLANES * edge_y, PLANES * edge_y)
-        mbzh[layer, :, :PLANES * edge_y] = banded(layer, 2, True, k % bz_len - i % bz_len + half, k // bz_len == i // bz_len)
-        i, k = grid(PLANES * edge_y, 2 * edge)
-        side, plane, depth, y = edge_index(k)
-        hop = depth + side * (bz_len + half) - i % bz_len
-        mbzh[layer, :, PLANES * edge_y:] = banded(layer, 2, True, hop, (plane == i // edge_y) & (y == i // bz_len % half))
-        wt[layer] = jnp.transpose(w[layer].astype(F32)).astype(BF16)
-
-    lax.fori_loop(0, num_layers, build_forward, 0)
-    i, k = grid(2 * edge, PLANES * edge_y)
-    side, plane, depth, y = edge_index(i)
-    z = depth + side * (bz_len - half)
-    sel[...] = jnp.where((k // edge_y == plane) & (k % edge_y == y * bz_len + z), 1.0, 0.0).astype(BF16)
-
     pl.semaphore_wait(barrier, group)
 
     def exchange(src, stage, tau):
         at = pl.ds(tau * PLANES, PLANES)
         y_near, z_near = {0: None, 1: y_hi, -1: y_lo}, {0: None, 1: z_hi, -1: z_lo}
         entries = []
-        for dy, dz in ((1, 0), (-1, 0), (0, 1), (0, -1), (1, 1), (1, -1), (-1, 1), (-1, -1)):
+        for dy, dz in ((1, 1), (1, -1), (-1, 1), (-1, -1), (1, 0), (-1, 0), (0, 1), (0, -1)):
             device = {}
             if dy:
                 device['gy'] = jnp.clip(my_y + dy, 0, ny - 1)
@@ -222,6 +153,74 @@
 
     for j in range(half):
         x_copy(vols, 0, 0, j).start()
+
+    def iota(shape, axis):
+        return lax.broadcasted_iota(jnp.int32, shape, axis)
+
+    def banded(layer, axis, back, hop, inside):
+        total = jnp.zeros(hop.shape, F32)
+        for t in range(num_taps):
+            tap = taps[layer, axis, num_taps - 1 - t if back else t]
+            if axis == 0:
+                tap = jnp.where(my_x == 1, tap, taps[layer, axis, t if back else num_taps - 1 - t])
+            total = jnp.where(hop == t, tap, total)
+        return jnp.where(inside, total, 0.0).astype(BF16)
+
+    def edge_index(e):
+        return e // edge, e % edge // (half * half), e % (half * half) // half, e % half
+
+    def grid(row_count, column_count):
+        return iota((row_count, column_count), 0), iota((row_count, column_count), 1)
+
+    def build_forward(layer, carry):
+        i, k = grid(PLANES * edge_y, (PLANES + 2 * half) * edge_y)
+        mfx[layer, :PLANES * edge_y] = banded(layer, 0, False, k // edge_y - i // edge_y, k % edge_y == i % edge_y)
+        i, k = grid(2 * edge, (PLANES + 2 * half) * edge_y)
+        side, plane, depth, y = edge_index(i)
+        z = depth + side * (bz_len - half)
+        mfx[layer, PLANES * edge_y:] = banded(layer, 0, False, k // edge_y - plane, k % edge_y == y * bz_len + z)
+        i, k = grid(half_rows, half_rows + 2 * edge_y)
+        mfy[layer] = banded(layer, 1, False, k // bz_len - i // bz_len, k % bz_len == i % bz_len)
+        i, k = grid(PLANES * half * by_len, (pairs + 2) * edge)
+        side, plane, depth, y = edge_index(k % edge)
+        y = (k // edge - 1) * half + y
+        i_y = i // (half * half_y) % 2 * half_y + i % half_y
+        inside = (plane == i // (half * by_len)) & (depth == i // half_y % half)
+        mfyh[layer] = banded(layer, 1, False, y - i_y + half, inside)
+        i, k = grid(half_rows, half_rows)
+        mfz[layer, :, :half_rows] = banded(layer, 2, False, k % bz_len - i % bz_len + half, k // bz_len == i // bz_len)
+        i, k = grid(half_rows, half * by_len)
+        hop = k // half_y % half + k // (half * half_y) * (bz_len + half) - i % bz_len
+        mfz[layer, :, half_rows:] = banded(layer, 2, False, hop, k % half_y == i // bz_len)
+        return carry
+
+    def build_backward(layer, tau):
+        i, k = grid(PLANES * edge_y, (PLANES + 2 * half) * edge_y)
+        mbx[layer] = banded(layer, 0, True, k // edge_y - i // edge_y, k % edge_y == i % edge_y)
+        i, k = grid(half_rows, half_rows + 2 * edge_y)
+        mby[layer] = banded(layer, 1, True, k // bz_len - i // bz_len, k % bz_len == i % bz_len)
+        i, k = grid(half_rows, half_rows)
+        own_back = banded(layer, 2, True, k % bz_len - i % bz_len + half, k // bz_len == i // bz_len)
+        i, k = grid(half_rows, pairs * edge)
+        side, (_, plane, depth, y) = k // (pairs * edge // 2), edge_index(k % edge)
+        y = k // edge % (pairs // 2) * half + y
+        hop = depth + side * (bz_len + half) - i % bz_len
+        for p in range(PLANES):
+            mbz[layer, p, :, :half_rows] = own_back
+            mbz[layer, p, :, half_rows:] = banded(layer, 2, True, hop, (y == i // bz_len) & (plane == p))
+        i, k = grid(PLANES * edge_y, PLANES * edge_y)
+        mbzh[layer, :, :PLANES * edge_y] = banded(layer, 2, True, k % bz_len - i % bz_len + half, k // bz_len == i // bz_len)
+        i, k = grid(PLANES * edge_y, 2 * edge)
+        side, plane, depth, y = edge_index(k)
+        hop = depth + side * (bz_len + half) - i % bz_len
+        mbzh[layer, :, PLANES * edge_y:] = banded(layer, 2, True, hop, (plane == i // edge_y) & (y == i // bz_len % half))
+        wt[layer] = jnp.transpose(w[layer].astype(F32)).astype(BF16)
+
+    lax.fori_loop(0, num_layers, build_forward, 0)
+    i, k = grid(2 * edge, PLANES * edge_y)
+    side, plane, depth, y = edge_index(i)
+    z = depth + side * (bz_len - half)
+    sel[...] = jnp.where((k // edge_y == plane) & (k % edge_y == y * bz_len + z), 1.0, 0.0).astype(BF16)
 
     for layer in range(num_layers):
         vols[layer, planes + half:] = jnp.zeros((half,) + vols.shape[2:], BF16)

time: 83.2 us -> 82.9 us (level)
  no operation moved by 1% of the time
where the time goes in v9:
time: 82.9 us; the launch traced here: 82.7 us
  Pallas kernels  82.1 us (99%)
    pallas_call x1, Pallas kernels, local_step(): pl.pallas_call(functools.partial(kernel, (nx, ny, nz, num_layers, num_tap...  80.5 us

profile of v9, /device:TPU:97, one launch (start us, length us, event | category | flops | bytes accessed | tf_op | source)
XLA Modules:
  0.0 82.7 jit_solution(12477613757359934658)
XLA Ops:
  0.6 80.5 %stack.1 = (bf16[16,256,256]{2,1,0:T(8,128)(2,1)S(1)}, f32[3,256,256]{2,1,0:T(8,128)S(1)}, f32[3,256]{1,0:T(4,128)S(1)}) custom-call(bf16[16,256,256]{2,1,0:T(8,128)(2,1)} %bitcast.9, bf16[16,256,256]{2,1,0:T(8,128)(2,1)} %bitcast.10, f32[3,3,5]{2,1,0:T(4,128)} %taps.1, bf16[3,256,256]{2,1,0:T(8,128)(2,1)} %w.1, f32[3,256]{1,0:T(4,128)} %b.1), custom_call_target="tpu_custom_call" | custom-call | tf_op jit(solution)/shard_map/stack/pallas_call | solution.py:496
  81.1 1.6 %write.1 = (bf16[16,256,256]{2,1,0:T(8,128)(2,1)}, f32[3,256,256]{2,1,0:T(8,128)}, f32[3,256]{1,0:T(4,128)}) custom-call(bf16[16,256,256]{2,1,0:T(8,128)(2,1)S(1)} %get-tuple-element.9.grad, f32[3,256,256]{2,1,0:T(8,128)S(1)} %get-tuple-element.10.gw, f32[3,256]{1,0:T(4,128)S(1)} %get-tuple-element.11.gb), custom_call_target="tpu_custom_call" | custom-call | tf_op jit(solution)/shard_map/write/pallas_call | solution.py:541

commit v10 on v9

--- a/solution.py
+++ b/solution.py
@@ -263,6 +263,8 @@
         return jnp.concatenate([buf[layer, tau * PLANES + p, at, :] for p in range(PLANES + 2 * half)], axis=0)
 
     def fx(layer, tau):
+        if layer == 0 and nt % 2 == 0:
+            tau = tau + 1 - 2 * lax.rem(tau, 2)
         wait_x(vols, layer, layer, tau)
         for group in range(pairs):
             total = dot(mfx[layer], x_source(vols, layer, tau, group)).astype(BF16)

time: 82.9 us -> 84 us (1.013)
  Pallas kernels: 82.1 us -> 83.2 us
    pallas_call x1, Pallas kernels: 80.5 us -> 81.6 us  [local_step(): pl.pallas_call(functools.partial(kernel, (nx, ny, nz, num_layers, num_tap...]
where the time goes in v10:
time: 84 us; the launch traced here: 83.8 us
  Pallas kernels  83.2 us (99%)
    pallas_call x1, Pallas kernels, local_step(): pl.pallas_call(functools.partial(kernel, (nx, ny, nz, num_layers, num_tap...  81.6 us

profile of v10, /device:TPU:97, one launch (start us, length us, event | category | flops | bytes accessed | tf_op | source)
XLA Modules:
  0.0 83.8 jit_solution(2262568984675813080)
XLA Ops:
  0.6 81.6 %stack.1 = (bf16[16,256,256]{2,1,0:T(8,128)(2,1)S(1)}, f32[3,256,256]{2,1,0:T(8,128)S(1)}, f32[3,256]{1,0:T(4,128)S(1)}) custom-call(bf16[16,256,256]{2,1,0:T(8,128)(2,1)} %bitcast.9, bf16[16,256,256]{2,1,0:T(8,128)(2,1)} %bitcast.10, f32[3,3,5]{2,1,0:T(4,128)} %taps.1, bf16[3,256,256]{2,1,0:T(8,128)(2,1)} %w.1, f32[3,256]{1,0:T(4,128)} %b.1), custom_call_target="tpu_custom_call" | custom-call | tf_op jit(solution)/shard_map/stack/pallas_call | solution.py:498
  82.2 1.6 %write.1 = (bf16[16,256,256]{2,1,0:T(8,128)(2,1)}, f32[3,256,256]{2,1,0:T(8,128)}, f32[3,256]{1,0:T(4,128)}) custom-call(bf16[16,256,256]{2,1,0:T(8,128)(2,1)S(1)} %get-tuple-element.9.grad, f32[3,256,256]{2,1,0:T(8,128)S(1)} %get-tuple-element.10.gw, f32[3,256]{1,0:T(4,128)S(1)} %get-tuple-element.11.gb), custom_call_target="tpu_custom_call" | custom-call | tf_op jit(solution)/shard_map/write/pallas_call | solution.py:543
